TPU v7x, 32 devices: a whole 2x2x4 slice. The times are simulated.
32 devices in a mesh: rows: 2 (over core), cols: 2 (over y), slabs: 2 (over x), site: 4 (over z).
Axes of the slice: x: 2, y: 2, z: 4, core: 2. Of those that a mesh axis runs over, the one named last changes fastest.
Arguments:
- field_values: float32 [768, 16, 16, 128], P(('site', 'rows'), 'cols', 'slabs'), parts along dimension 0, may hold values from 0.5 to 2
- crowding: float32 [768, 16, 16, 128], P(('site', 'rows'), 'cols', 'slabs'), parts along dimension 0, may hold values from 0.5 to 2
Outputs:
- standardized: float32 [768, 16, 16, 128], P(('site', 'rows'), 'cols', 'slabs'), parts along dimension 0
- field_values_end: float32 [768, 16, 16, 128], P(('site', 'rows'), 'cols', 'slabs'), parts along dimension 0
There are 4 independent parts, one for each index of `site`. A program takes and returns all parts, laid end to end along the dimension named above; each array names one. Nothing has to cross between parts.
All inputs are finite; a program needn't handle non-finite values.
Results may differ from a plain program's by a relative error of at most 0.000036.
Values sent between devices are 32-bit elements; how exact they have to be, the bound alone decides.
No kernel may reach another device: no remote copies, remote signals or barrier semaphores. Data moves between devices by JAX's collectives and lax.ppermute only.
A program may use at most 64 MiB of HBM per device.

v0:
```python
import functools

import jax
import jax.numpy as jnp
from jax import lax
from jax.experimental import pallas as pl
from jax.experimental.pallas import tpu as pltpu
from jax.sharding import PartitionSpec as P


STEPS = 6
CHUNKS = (1, 1, 1)
EPS = 0.0001
VMEM_GRANT = 16 << 20


VMEM_SPEC = pl.BlockSpec(memory_space=pltpu.VMEM)
ANY_SPEC = pl.BlockSpec(memory_space=pl.ANY)
PARAMS = pltpu.CompilerParams(vmem_limit_bytes=VMEM_GRANT)


def in_vmem(value):
    return pltpu.with_memory_space_constraint(value, pltpu.VMEM)


def in_hbm(value):
    return pltpu.with_memory_space_constraint(value, pltpu.HBM)


def vmem_out(*shape):
    return pltpu.VMEM(shape, jnp.float32)


def cost(shape, flops_per_cell, arrays):
    cells = 1
    for size in shape:
        cells *= size
    return pl.CostEstimate(flops=flops_per_cell * cells, bytes_accessed=4 * arrays * cells, transcendentals=0)


def split(length, shares):
    edges = [length * sum(shares[:i]) // sum(shares) for i in range(len(shares) + 1)]
    return [(a, b - a) for a, b in zip(edges[:-1], edges[1:]) if b > a]


def store_faces(row, planes, x_low, x_high, z_faces):
    last_x, last_z = len(planes) - 1, planes[0].shape[0] - 1
    x_low[row] = planes[0]
    x_high[row] = planes[last_x]
    at = 0
    for z_face in z_faces:
        for x in range(z_face.shape[2]):
            z_face[0, row, x:x + 1, :] = planes[at + x][0:1, :]
            z_face[1, row, x:x + 1, :] = planes[at + x][last_z:last_z + 1, :]
        at += z_face.shape[2]


def open_kernel(start, parts, whole, after, field, y_first, y_last, x_face, z_face, sems):
    rows, xs = field.shape[0], field.shape[1]
    copies = [
        pltpu.make_async_copy(whole.at[pl.ds(start + at, size)], field.at[pl.ds(at, size)], sems.at[part])
        for part, (at, size) in enumerate(parts)
    ]
    for copy in copies:
        copy.start()

    def row_faces(row, carry):
        store_faces(row, [field[row, x] for x in range(xs)], x_face.at[0], x_face.at[1], [z_face])
        return carry

    for copy, (at, size) in zip(copies, parts):
        copy.wait()
        lax.fori_loop(at, at + size, row_faces, 0, unroll=4)
    y_first[...] = field[0]
    y_last[...] = field[rows - 1]


def open_chunk(field_values, after, start, rows):
    _, xs, zs, levels = field_values.shape
    parts = split(rows, (1,) * 4)
    outs = [vmem_out(rows, xs, zs, levels), vmem_out(xs, zs, levels), vmem_out(xs, zs, levels)]
    outs += [vmem_out(2, rows, zs, levels), vmem_out(2, rows, xs, levels)]
    return pl.pallas_call(
        functools.partial(open_kernel, start, parts),
        out_shape=tuple(outs),
        in_specs=[ANY_SPEC] * 2,
        out_specs=(VMEM_SPEC,) * len(outs),
        scratch_shapes=[pltpu.SemaphoreType.DMA((len(parts),))],
        compiler_params=PARAMS,
        cost_estimate=cost((rows, xs, zs, levels), 4, 2),
        name="open_chunk",
    )(in_hbm(field_values), after)


def update_rows(start, span, field, crowding, y_before, y_after, x_before, x_after, z_before, z_after,
                out, finish, total):
    rows, xs, zs, levels = field.shape
    x0, x1 = span
    place = lax.broadcasted_iota(jnp.int32, (zs, levels), 0)
    is_first, is_last = place == 0, place == zs - 1

    def planes(ref, row):
        return [ref[row, x] for x in range(x0, x1)]

    def advance(row, below, here, above, total):
        first = x_before[row] if x0 == 0 else field[row, x0 - 1]
        final = x_after[row] if x1 == xs else field[row, x1]
        along = [first, *here, final]
        new = []
        for i, u in enumerate(here):
            near = jnp.broadcast_to(z_before[row, i:i + 1, :], (zs, levels))
            far = jnp.broadcast_to(z_after[row, i:i + 1, :], (zs, levels))
            near = jnp.where(is_first, near, pltpu.roll(u, 1, 0))
            far = jnp.where(is_last, far, pltpu.roll(u, zs - 1, 0))
            around = (along[i] + along[i + 2]) + (near + far) + (below[i] + above[i])
            new.append(0.1 * around + u * (0.6 - 0.2 * (u * crowding[start + row, x0 + i])))
        for i, u in enumerate(new):
            out[row, i] = u
        return finish(row, new, total)

    def body(row, total):
        return advance(row, planes(field, row - 1), planes(field, row), planes(field, row + 1), total)

    top = [y_before[x] for x in range(x0, x1)]
    bottom = [y_after[x] for x in range(x0, x1)]
    total = advance(0, top, planes(field, 0), planes(field, 1), total)
    total = lax.fori_loop(1, rows - 1, body, total, unroll=3 * xs // (x1 - x0))
    return advance(rows - 1, planes(field, rows - 2), planes(field, rows - 1), bottom, total)


def sides(halo):
    return (halo[0].at[1], halo[0].at[0]) if len(halo) == 1 else tuple(halo)


def step_kernel(start, x_count, z_count, halves, gathers, *refs):
    field, crowding, y_before, y_after = refs[:4]
    x_before, x_after = sides(refs[4:4 + x_count])
    z_before, z_after = sides(refs[4 + x_count:4 + x_count + z_count])
    held = refs[5 + x_count + z_count:5 + x_count + z_count + 2 * gathers]
    outs = refs[5 + x_count + z_count + 2 * gathers:]
    out, y_first, y_last = outs[:3]
    if halves:
        x_low, x_high, *z_faces = outs[3:7]
    else:
        x_face, *z_faces = outs[3:]
        x_low, x_high = x_face.at[0], x_face.at[1]

    def finish(row, new, total):
        store_faces(row, new, x_low, x_high, z_faces)
        return total

    update_rows(start, (0, field.shape[1]), field, crowding, y_before, y_after, x_before, x_after,
                z_before, z_after, out, finish, 0)
    y_first[...] = out[0]
    y_last[...] = out[field.shape[0] - 1]
    if gathers:
        x_all, z_all = outs[7:]
        at = 0
        for low, face in zip(held[:gathers], held[gathers:]):
            rows = low.shape[0]
            x_all[at:at + rows] = low[...]
            z_all[:, at:at + rows] = face[...]
            at += rows


def step_chunk(field, crowding, y_before, y_after, x_halo, z_halo, start, after, halves, held):
    rows, xs, zs, levels = field.shape
    gathers = len(held)
    operands = [field, crowding, y_before, y_after, *x_halo, *z_halo, after]
    operands += [low for low, _ in held] + [face for _, face in held]
    outs = [vmem_out(rows, xs, zs, levels), vmem_out(xs, zs, levels), vmem_out(xs, zs, levels)]
    if halves:
        cut = half(xs)
        outs += [vmem_out(rows, zs, levels)] * 2
        outs += [vmem_out(2, rows, cut, levels), vmem_out(2, rows, xs - cut, levels)]
        if gathers:
            outs += [vmem_out(start, zs, levels), vmem_out(2, start, xs - cut, levels)]
    else:
        outs += [vmem_out(2, rows, zs, levels), vmem_out(2, rows, xs, levels)]
    return pl.pallas_call(
        functools.partial(step_kernel, start, len(x_halo), len(z_halo), halves, gathers),
        out_shape=tuple(outs),
        in_specs=[VMEM_SPEC] * len(operands),
        out_specs=(VMEM_SPEC,) * len(outs),
        compiler_params=PARAMS,
        cost_estimate=cost((rows, xs, zs, levels), 16, 3),
        name="step",
    )(*[in_vmem(operand) for operand in operands])


def half(xs):
    return xs // 2


def merge(groups):
    count, mean, square = groups[0]
    for other_count, other_mean, other_square in groups[1:]:
        both = count + other_count
        apart = other_mean - mean
        mean = mean + apart * (other_count / both)
        square = square + other_square + (apart * apart) * (count * other_count / both)
        count = both
    return count, mean, square


def last_kernel(start, span, halo_at, z_count, earlier, waits, *refs):
    field, crowding, y_before, y_after, x_halo = refs[:5]
    x0, x1 = span
    rows = field.shape[0]
    here = pl.ds(halo_at, rows)
    x_side = x_halo.at[here]
    z_before, z_after = [side.at[here] for side in sides(refs[5:5 + z_count])]
    rest = refs[5 + z_count:]
    earlier_stats = rest[0] if earlier else None
    out, stats = rest[earlier + waits:]

    def finish(row, new, total):
        if total is None:
            return new, [jnp.zeros_like(u) for u in new], [jnp.zeros_like(u) for u in new]
        base, sums, squares = total
        away = [u - b for u, b in zip(new, base)]
        sums = [s + d for s, d in zip(sums, away)]
        squares = [q + d * d for q, d in zip(squares, away)]
        return base, sums, squares

    base, sums, squares = update_rows(
        start, span, field, crowding, y_before, y_after, x_side, x_side, z_before, z_after,
        out, finish, None)
    for i in range(x1 - x0):
        mean = base[i] + sums[i] * (1.0 / rows)
        square = squares[i] - sums[i] * sums[i] * (1.0 / rows)
        groups = [(rows, mean, square)]
        if earlier:
            groups = [(start, earlier_stats[0, i], earlier_stats[1, i])] + groups
        _, stats[0, i], stats[1, i] = merge(groups)


def last_chunk(field, crowding, y_before, y_after, x_halo, z_halo, start, span, halo_at, earlier_stats, wait):
    rows, _, zs, levels = field.shape
    wide = span[1] - span[0]
    operands = [in_vmem(v) for v in (field, crowding, y_before, y_after, x_halo, *z_halo)]
    specs = [VMEM_SPEC] * len(operands)
    if earlier_stats is not None:
        operands.append(in_vmem(earlier_stats))
        specs.append(VMEM_SPEC)
    if wait is not None:
        operands.append(in_hbm(wait))
        specs.append(ANY_SPEC)
    return pl.pallas_call(
        functools.partial(
            last_kernel, start, span, halo_at, len(z_halo), earlier_stats is not None, wait is not None),
        out_shape=(vmem_out(rows, wide, zs, levels), vmem_out(2, wide, zs, levels)),
        in_specs=specs,
        out_specs=(VMEM_SPEC,) * 2,
        compiler_params=PARAMS,
        cost_estimate=cost((rows, wide, zs, levels), 20, 3),
        name="last_step",
    )(*operands)


def part_copies(parts, starts, span, end, sems):
    return [
        pltpu.make_async_copy(
            part, end.at[pl.ds(start, part.shape[0]), pl.ds(span[0], part.shape[1])], sems.at[c])
        for c, (part, start) in enumerate(zip(parts, starts))
    ]


def write_kernel(starts, span, *refs):
    chunks = len(starts)
    end, sems = refs[-2:]
    copies = part_copies(refs[:chunks], starts, span, end, sems)
    for copy in copies:
        copy.start()
    for copy in copies:
        copy.wait()


def write_parts(parts, starts, span, end):
    return pl.pallas_call(
        functools.partial(write_kernel, starts, span),
        out_shape=jax.ShapeDtypeStruct(end.shape, end.dtype),
        in_specs=[VMEM_SPEC] * len(parts) + [ANY_SPEC],
        out_specs=ANY_SPEC,
        input_output_aliases={len(parts): 0},
        scratch_shapes=[pltpu.SemaphoreType.DMA((len(parts),))],
        compiler_params=PARAMS,
        cost_estimate=cost(parts[0].shape, 4 * len(parts), 2),
        name="write_parts",
    )(*[in_vmem(part) for part in parts], end)


def close_kernel(starts, span, others, pieces, first, *refs):
    chunks = len(starts)
    parts = refs[:chunks]
    stats = refs[chunks:chunks + 1 + others]
    copies = []
    if first:
        scaled, end, stage, sems, end_sems = refs[chunks + 1 + others:]
        copies = part_copies(parts, starts, span, end, end_sems)
        for copy in copies:
            copy.start()
    else:
        scaled, stage, sems = refs[chunks + 2 + others:]
    x0, x1 = span
    wide = x1 - x0
    length = stage.shape[0]
    means, gains = [], []
    for i in range(wide):
        count, mean, square = merge([(length, s[0, i], s[1, i]) for s in stats])
        means.append(mean)
        gains.append(lax.rsqrt(square * (1.0 / count) + EPS))
    for piece, (c, at, size) in enumerate(pieces):
        base = starts[c]

        def scale(row, carry, part=parts[c], base=base):
            for i in range(wide):
                stage[base + row, i] = (part[row, i] - means[i]) * gains[i]
            return carry

        lax.fori_loop(at, at + size, scale, 0, unroll=8)
        copy = pltpu.make_async_copy(
            stage.at[pl.ds(base + at, size)], scaled.at[pl.ds(base + at, size), pl.ds(x0, wide)], sems.at[piece])
        copy.start()
        copies.append(copy)
    for copy in copies:
        copy.wait()


def close(parts, starts, span, stats, shape, scaled):
    first = scaled is None
    length, _, zs, levels = shape
    wide = span[1] - span[0]
    whole = jax.ShapeDtypeStruct(shape, jnp.float32)
    pieces = [(c, at, size) for c, f in enumerate(parts) for at, size in split(f.shape[0], (1,) * 2)]
    operands = [in_vmem(v) for v in (*parts, *stats)]
    specs = [VMEM_SPEC] * len(operands)
    if not first:
        operands.append(scaled)
        specs.append(ANY_SPEC)
    outs = (whole, whole) if first else (whole,)
    scratch = [pltpu.VMEM((length, wide, zs, levels), jnp.float32), pltpu.SemaphoreType.DMA((len(pieces),))]
    return pl.pallas_call(
        functools.partial(close_kernel, starts, span, len(stats) - 1, pieces, first),
        out_shape=outs,
        in_specs=specs,
        out_specs=(ANY_SPEC,) * len(outs),
        input_output_aliases={} if first else {len(operands) - 1: 0},
        scratch_shapes=scratch + ([pltpu.SemaphoreType.DMA((len(parts),))] if first else []),
        compiler_params=PARAMS,
        cost_estimate=cost((length, wide, zs, levels), 3, 4),
        name="close",
    )(*operands)


def ring(axis):
    devices = lax.axis_size(axis)
    up = [(i, (i + 1) % devices) for i in range(devices)]
    return devices, up, [(j, i) for i, j in up]


def exchange(face, axis):
    devices, up, down = ring(axis)
    if devices <= 2:
        return (lax.ppermute(face, axis, up),)
    return (lax.ppermute(face[1], axis, up), lax.ppermute(face[0], axis, down))


def local(field_values, crowding):
    length, xs = field_values.shape[:2]
    pieces = split(length, CHUNKS)
    starts = [start for start, _ in pieces]
    chunks = len(pieces)
    devices, up, down = ring("rows")
    _, x_up, x_down = ring("cols")
    state = []
    for start, rows in pieces:
        state.append(open_chunk(field_values, state[-1][1] if state else field_values, start, rows))
    for step in range(STEPS - 1):
        halos = [(exchange(s[3], "cols"), exchange(s[4], "slabs")) for s in state]
        before = lax.ppermute(state[-1][2], "rows", up)
        after = lax.ppermute(state[0][1], "rows", down)
        new = []
        for c, (s, (x_halo, z_halo), start) in enumerate(zip(state, halos, starts)):
            y_before = before if c == 0 else state[c - 1][2]
            y_after = after if c == chunks - 1 else state[c + 1][1]
            halves = step == STEPS - 2
            held = [(n[3], n[6]) for n in new] if halves and c == chunks - 1 else []
            new.append(step_chunk(s[0], crowding, y_before, y_after, x_halo, z_halo, start,
                                  new[-1][1] if new else s[1], halves, held))
        state = new
    before = lax.ppermute(state[-1][2], "rows", up)
    after = lax.ppermute(state[0][1], "rows", down)
    hops = [[(i, (i + hop) % devices) for i in range(devices)] for hop in range(1, devices)]
    cut = half(xs)
    low_span, high_span = (0, cut), (cut, xs)

    def last_half(span, x_halos, z_halos, offsets, wait):
        parts, stats = [], None
        for c, s in enumerate(state):
            y_before = before if c == 0 else state[c - 1][2]
            y_after = after if c == chunks - 1 else state[c + 1][1]
            part, stats = last_chunk(
                s[0], crowding, y_before, y_after, x_halos[c], z_halos[c], starts[c], span, offsets[c], stats,
                wait if c == chunks - 1 else None)
            parts.append(part)
        return parts, [stats, *[lax.ppermute(stats, "rows", hop) for hop in hops]]

    def send(x_face, pairs, z_face):
        x_halo = lax.ppermute(x_face, "cols", pairs)
        return x_halo, exchange(z_face, "slabs")

    halos = [send(s[4], x_up, s[5]) for s in state]
    low, low_stats = last_half(low_span, *zip(*halos), [0] * chunks, None)
    scaled, end = close(low, starts, low_span, low_stats, field_values.shape, None)
    halos = [send(state[-1][3], x_down, state[-1][6])]
    if chunks > 1:
        halos = [send(state[-1][7], x_down, state[-1][8])] * (chunks - 1) + halos
    high, high_stats = last_half(high_span, *zip(*halos), [*starts[:-1], 0], scaled)
    end = write_parts(high, starts, high_span, end)
    (scaled,) = close(high, starts, high_span, high_stats, field_values.shape, scaled)
    return scaled, end


def solution(mesh):
    spec = P(("site", "rows"), "cols", "slabs", None)

    return jax.shard_map(local, mesh=mesh, in_specs=(spec, spec), out_specs=(spec, spec), check_vma=False)
```

profile of v0, /device:TPU:0, one launch (start us, length us, event | category | flops | bytes accessed | tf_op | source)
XLA Modules:
  0.0 117.2 jit_solution(4016110102413885170)
XLA Ops:
  0.6 1.3 %open_chunk.3 = (f32[32,8,8,128]{3,2,1,0:T(8,128)S(1)}, f32[8,8,128]{2,1,0:T(8,128)S(1)}, f32[8,8,128]{2,1,0:T(8,128)S(1)}, f32[2,32,8,128]{3,2,1,0:T(8,128)S(1)}, f32[2,32,8,128]{3,2,1,0:T(8,128)S(1)}) custom-call(f32[96,8,8,128]{3,2,1,0:T(8,128)} %whole.5, f32[96,8,8,128]{3,2,1,0:T(8,128)} %whole.5), custom_call_target="tpu_custom_call" | custom-call | flops 1048576 | bytes 2097152 | tf_op jit(solution)/shard_map/open_chunk/pallas_call | solution.py:83
  1.9 3.1 %collective-permute-start.1 = (f32[2,32,8,128]{3,2,1,0:T(8,128)S(1)}, f32[2,32,8,128]{3,2,1,0:T(8,128)S(1)}, u32[]{:S(2)}, u32[]{:S(2)}) collective-permute-start(f32[2,32,8,128]{3,2,1,0:T(8,128)S(1)} %get-tuple-element.118), channel_id=1, source_target_pairs={{0,8},{8,0},{1,9},{9,1},{2,10},{10,2},{3,11},{11,3},{4,12},{12,4},... | collective-permute-start | bytes 786440 | tf_op jit(solution)/shard_map/ppermute | solution.py:365
  5.0 1.5 %collective-permute-start.2 = (f32[2,32,8,128]{3,2,1,0:T(8,128)S(1)}, f32[2,32,8,128]{3,2,1,0:T(8,128)S(1)}, u32[]{:S(2)}, u32[]{:S(2)}) collective-permute-start(f32[2,32,8,128]{3,2,1,0:T(8,128)S(1)} %get-tuple-element.119), channel_id=1, source_target_pairs={{0,4},{4,0},{1,5},{5,1},{2,6},{6,2},{3,7},{7,3},{8,12},{12,8},{9,1... | collective-permute-start | bytes 786440 | tf_op jit(solution)/shard_map/ppermute | solution.py:365
  6.5 1.4 %open_chunk.4 = (f32[32,8,8,128]{3,2,1,0:T(8,128)S(1)}, f32[8,8,128]{2,1,0:T(8,128)S(1)}, f32[8,8,128]{2,1,0:T(8,128)S(1)}, f32[2,32,8,128]{3,2,1,0:T(8,128)S(1)}, f32[2,32,8,128]{3,2,1,0:T(8,128)S(1)}) custom-call(f32[96,8,8,128]{3,2,1,0:T(8,128)} %whole.5, f32[8,8,128]{2,1,0:T(8,128)S(1)} %get-tuple-element.115.after.refs_6_), custom_call_target="tpu_custom_call" | custom-call | flops 1048576 | bytes 2097152 | tf_op jit(solution)/shard_map/open_chunk/pallas_call | solution.py:83
  8.6 1.3 %open_chunk.5 = (f32[32,8,8,128]{3,2,1,0:T(8,128)S(1)}, f32[8,8,128]{2,1,0:T(8,128)S(1)}, f32[8,8,128]{2,1,0:T(8,128)S(1)}, f32[2,32,8,128]{3,2,1,0:T(8,128)S(1)}, f32[2,32,8,128]{3,2,1,0:T(8,128)S(1)}) custom-call(f32[96,8,8,128]{3,2,1,0:T(8,128)} %whole.5, f32[8,8,128]{2,1,0:T(8,128)S(1)} %get-tuple-element.116.after.refs_3_), custom_call_target="tpu_custom_call" | custom-call | flops 1048576 | bytes 2097152 | tf_op jit(solution)/shard_map/open_chunk/pallas_call | solution.py:83
  9.9 1.2 %collective-permute-done.refs_2_ = f32[8,8,128]{2,1,0:T(8,128)S(1)} collective-permute-done((f32[8,8,128]{2,1,0:T(8,128)S(1)}, f32[8,8,128]{2,1,0:T(8,128)S(1)}, u32[]{:S(2)}, u32[]{:S(2)}) %collective-permute-start) | collective-permute-done | bytes 32800 | tf_op jit(solution)/shard_map/ppermute | solution.py:381
  11.1 1.9 %collective-permute-start.4 = (f32[2,32,8,128]{3,2,1,0:T(8,128)S(1)}, f32[2,32,8,128]{3,2,1,0:T(8,128)S(1)}, u32[]{:S(2)}, u32[]{:S(2)}) collective-permute-start(f32[2,32,8,128]{3,2,1,0:T(8,128)S(1)} %get-tuple-element.123), channel_id=1, source_target_pairs={{0,8},{8,0},{1,9},{9,1},{2,10},{10,2},{3,11},{11,3},{4,12},{12,4},... | collective-permute-start | bytes 786440 | tf_op jit(solution)/shard_map/ppermute | solution.py:365
  13.1 1.5 %collective-permute-start.5 = (f32[2,32,8,128]{3,2,1,0:T(8,128)S(1)}, f32[2,32,8,128]{3,2,1,0:T(8,128)S(1)}, u32[]{:S(2)}, u32[]{:S(2)}) collective-permute-start(f32[2,32,8,128]{3,2,1,0:T(8,128)S(1)} %get-tuple-element.124), channel_id=1, source_target_pairs={{0,4},{4,0},{1,5},{5,1},{2,6},{6,2},{3,7},{7,3},{8,12},{12,8},{9,1... | collective-permute-start | bytes 786440 | tf_op jit(solution)/shard_map/ppermute | solution.py:365
  16.3 1.4 %collective-permute-done.6.refs_4_ = f32[2,32,8,128]{3,2,1,0:T(8,128)S(1)} collective-permute-done((f32[2,32,8,128]{3,2,1,0:T(8,128)S(1)}, f32[2,32,8,128]{3,2,1,0:T(8,128)S(1)}, u32[]{:S(2)}, u32[]{:S(2)}) %collective-permute-start.6) | collective-permute-done | bytes 262176 | tf_op jit(solution)/shard_map/ppermute | solution.py:365
  17.7 2.0 %collective-permute-start.10 = (f32[2,32,8,128]{3,2,1,0:T(8,128)S(1)}, f32[2,32,8,128]{3,2,1,0:T(8,128)S(1)}, u32[]{:S(2)}, u32[]{:S(2)}) collective-permute-start(f32[2,32,8,128]{3,2,1,0:T(8,128)S(1)} %get-tuple-element.134), channel_id=1, source_target_pairs={{0,4},{4,0},{1,5},{5,1},{2,6},{6,2},{3,7},{7,3},{8,12},{12,8},{9,1... | collective-permute-start | bytes 786440 | tf_op jit(solution)/shard_map/ppermute | solution.py:365
  21.0 1.5 %collective-permute-start.14 = (f32[2,32,8,128]{3,2,1,0:T(8,128)S(1)}, f32[2,32,8,128]{3,2,1,0:T(8,128)S(1)}, u32[]{:S(2)}, u32[]{:S(2)}) collective-permute-start(f32[2,32,8,128]{3,2,1,0:T(8,128)S(1)} %get-tuple-element.143), channel_id=1, source_target_pairs={{0,8},{8,0},{1,9},{9,1},{2,10},{10,2},{3,11},{11,3},{4,12},{12,4},... | collective-permute-start | bytes 786440 | tf_op jit(solution)/shard_map/ppermute | solution.py:365
  23.4 2.0 %collective-permute-start.15 = (f32[2,32,8,128]{3,2,1,0:T(8,128)S(1)}, f32[2,32,8,128]{3,2,1,0:T(8,128)S(1)}, u32[]{:S(2)}, u32[]{:S(2)}) collective-permute-start(f32[2,32,8,128]{3,2,1,0:T(8,128)S(1)} %get-tuple-element.144), channel_id=1, source_target_pairs={{0,4},{4,0},{1,5},{5,1},{2,6},{6,2},{3,7},{7,3},{8,12},{12,8},{9,1... | collective-permute-start | bytes 786440 | tf_op jit(solution)/shard_map/ppermute | solution.py:365
  26.1 1.2 %collective-permute-done.8.refs_2_ = f32[8,8,128]{2,1,0:T(8,128)S(1)} collective-permute-done((f32[8,8,128]{2,1,0:T(8,128)S(1)}, f32[8,8,128]{2,1,0:T(8,128)S(1)}, u32[]{:S(2)}, u32[]{:S(2)}) %collective-permute-start.8) | collective-permute-done | bytes 32800 | tf_op jit(solution)/shard_map/ppermute | solution.py:381
  27.3 1.5 %collective-permute-start.12 = (f32[2,32,8,128]{3,2,1,0:T(8,128)S(1)}, f32[2,32,8,128]{3,2,1,0:T(8,128)S(1)}, u32[]{:S(2)}, u32[]{:S(2)}) collective-permute-start(f32[2,32,8,128]{3,2,1,0:T(8,128)S(1)} %get-tuple-element.138), channel_id=1, source_target_pairs={{0,8},{8,0},{1,9},{9,1},{2,10},{10,2},{3,11},{11,3},{4,12},{12,4},... | collective-permute-start | bytes 786440 | tf_op jit(solution)/shard_map/ppermute | solution.py:365
  29.0 2.0 %collective-permute-start.13 = (f32[2,32,8,128]{3,2,1,0:T(8,128)S(1)}, f32[2,32,8,128]{3,2,1,0:T(8,128)S(1)}, u32[]{:S(2)}, u32[]{:S(2)}) collective-permute-start(f32[2,32,8,128]{3,2,1,0:T(8,128)S(1)} %get-tuple-element.139), channel_id=1, source_target_pairs={{0,4},{4,0},{1,5},{5,1},{2,6},{6,2},{3,7},{7,3},{8,12},{12,8},{9,1... | collective-permute-start | bytes 786440 | tf_op jit(solution)/shard_map/ppermute | solution.py:365
  31.6 1.6 %collective-permute-start.17 = (f32[2,32,8,128]{3,2,1,0:T(8,128)S(1)}, f32[2,32,8,128]{3,2,1,0:T(8,128)S(1)}, u32[]{:S(2)}, u32[]{:S(2)}) collective-permute-start(f32[2,32,8,128]{3,2,1,0:T(8,128)S(1)} %get-tuple-element.148), channel_id=1, source_target_pairs={{0,8},{8,0},{1,9},{9,1},{2,10},{10,2},{3,11},{11,3},{4,12},{12,4},... | collective-permute-start | bytes 786440 | tf_op jit(solution)/shard_map/ppermute | solution.py:365
  33.2 1.4 %collective-permute-done.14.refs_4_ = f32[2,32,8,128]{3,2,1,0:T(8,128)S(1)} collective-permute-done((f32[2,32,8,128]{3,2,1,0:T(8,128)S(1)}, f32[2,32,8,128]{3,2,1,0:T(8,128)S(1)}, u32[]{:S(2)}, u32[]{:S(2)}) %collective-permute-start.14) | collective-permute-done | bytes 262176 | tf_op jit(solution)/shard_map/ppermute | solution.py:365
  34.6 2.0 %collective-permute-start.18 = (f32[2,32,8,128]{3,2,1,0:T(8,128)S(1)}, f32[2,32,8,128]{3,2,1,0:T(8,128)S(1)}, u32[]{:S(2)}, u32[]{:S(2)}) collective-permute-start(f32[2,32,8,128]{3,2,1,0:T(8,128)S(1)} %get-tuple-element.149), channel_id=1, source_target_pairs={{0,4},{4,0},{1,5},{5,1},{2,6},{6,2},{3,7},{7,3},{8,12},{12,8},{9,1... | collective-permute-start | bytes 786440 | tf_op jit(solution)/shard_map/ppermute | solution.py:365
  37.8 1.5 %collective-permute-start.22 = (f32[2,32,8,128]{3,2,1,0:T(8,128)S(1)}, f32[2,32,8,128]{3,2,1,0:T(8,128)S(1)}, u32[]{:S(2)}, u32[]{:S(2)}) collective-permute-start(f32[2,32,8,128]{3,2,1,0:T(8,128)S(1)} %get-tuple-element.158), channel_id=1, source_target_pairs={{0,8},{8,0},{1,9},{9,1},{2,10},{10,2},{3,11},{11,3},{4,12},{12,4},... | collective-permute-start | bytes 786440 | tf_op jit(solution)/shard_map/ppermute | solution.py:365
  40.2 2.0 %collective-permute-start.23 = (f32[2,32,8,128]{3,2,1,0:T(8,128)S(1)}, f32[2,32,8,128]{3,2,1,0:T(8,128)S(1)}, u32[]{:S(2)}, u32[]{:S(2)}) collective-permute-start(f32[2,32,8,128]{3,2,1,0:T(8,128)S(1)} %get-tuple-element.159), channel_id=1, source_target_pairs={{0,4},{4,0},{1,5},{5,1},{2,6},{6,2},{3,7},{7,3},{8,12},{12,8},{9,1... | collective-permute-start | bytes 786440 | tf_op jit(solution)/shard_map/ppermute | solution.py:365
  42.9 1.2 %collective-permute-done.16.refs_2_ = f32[8,8,128]{2,1,0:T(8,128)S(1)} collective-permute-done((f32[8,8,128]{2,1,0:T(8,128)S(1)}, f32[8,8,128]{2,1,0:T(8,128)S(1)}, u32[]{:S(2)}, u32[]{:S(2)}) %collective-permute-start.16) | collective-permute-done | bytes 32800 | tf_op jit(solution)/shard_map/ppermute | solution.py:381
  44.1 1.5 %collective-permute-start.20 = (f32[2,32,8,128]{3,2,1,0:T(8,128)S(1)}, f32[2,32,8,128]{3,2,1,0:T(8,128)S(1)}, u32[]{:S(2)}, u32[]{:S(2)}) collective-permute-start(f32[2,32,8,128]{3,2,1,0:T(8,128)S(1)} %get-tuple-element.153), channel_id=1, source_target_pairs={{0,8},{8,0},{1,9},{9,1},{2,10},{10,2},{3,11},{11,3},{4,12},{12,4},... | collective-permute-start | bytes 786440 | tf_op jit(solution)/shard_map/ppermute | solution.py:365
  45.8 2.0 %collective-permute-start.21 = (f32[2,32,8,128]{3,2,1,0:T(8,128)S(1)}, f32[2,32,8,128]{3,2,1,0:T(8,128)S(1)}, u32[]{:S(2)}, u32[]{:S(2)}) collective-permute-start(f32[2,32,8,128]{3,2,1,0:T(8,128)S(1)} %get-tuple-element.154), channel_id=1, source_target_pairs={{0,4},{4,0},{1,5},{5,1},{2,6},{6,2},{3,7},{7,3},{8,12},{12,8},{9,1... | collective-permute-start | bytes 786440 | tf_op jit(solution)/shard_map/ppermute | solution.py:365
  48.5 1.6 %collective-permute-start.25 = (f32[2,32,8,128]{3,2,1,0:T(8,128)S(1)}, f32[2,32,8,128]{3,2,1,0:T(8,128)S(1)}, u32[]{:S(2)}, u32[]{:S(2)}) collective-permute-start(f32[2,32,8,128]{3,2,1,0:T(8,128)S(1)} %get-tuple-element.163), channel_id=1, source_target_pairs={{0,8},{8,0},{1,9},{9,1},{2,10},{10,2},{3,11},{11,3},{4,12},{12,4},... | collective-permute-start | bytes 786440 | tf_op jit(solution)/shard_map/ppermute | solution.py:365
  50.0 1.4 %collective-permute-done.22.refs_4_ = f32[2,32,8,128]{3,2,1,0:T(8,128)S(1)} collective-permute-done((f32[2,32,8,128]{3,2,1,0:T(8,128)S(1)}, f32[2,32,8,128]{3,2,1,0:T(8,128)S(1)}, u32[]{:S(2)}, u32[]{:S(2)}) %collective-permute-start.22) | collective-permute-done | bytes 262176 | tf_op jit(solution)/shard_map/ppermute | solution.py:365
  51.4 2.0 %collective-permute-start.26 = (f32[2,32,8,128]{3,2,1,0:T(8,128)S(1)}, f32[2,32,8,128]{3,2,1,0:T(8,128)S(1)}, u32[]{:S(2)}, u32[]{:S(2)}) collective-permute-start(f32[2,32,8,128]{3,2,1,0:T(8,128)S(1)} %get-tuple-element.164), channel_id=1, source_target_pairs={{0,4},{4,0},{1,5},{5,1},{2,6},{6,2},{3,7},{7,3},{8,12},{12,8},{9,1... | collective-permute-start | bytes 786440 | tf_op jit(solution)/shard_map/ppermute | solution.py:365
  54.7 1.5 %collective-permute-start.30 = (f32[2,32,8,128]{3,2,1,0:T(8,128)S(1)}, f32[2,32,8,128]{3,2,1,0:T(8,128)S(1)}, u32[]{:S(2)}, u32[]{:S(2)}) collective-permute-start(f32[2,32,8,128]{3,2,1,0:T(8,128)S(1)} %get-tuple-element.173), channel_id=1, source_target_pairs={{0,8},{8,0},{1,9},{9,1},{2,10},{10,2},{3,11},{11,3},{4,12},{12,4},... | collective-permute-start | bytes 786440 | tf_op jit(solution)/shard_map/ppermute | solution.py:365
  57.1 2.0 %collective-permute-done.21.refs_5_ = f32[2,32,8,128]{3,2,1,0:T(8,128)S(1)} collective-permute-done((f32[2,32,8,128]{3,2,1,0:T(8,128)S(1)}, f32[2,32,8,128]{3,2,1,0:T(8,128)S(1)}, u32[]{:S(2)}, u32[]{:S(2)}) %collective-permute-start.21) | collective-permute-done | bytes 262176 | tf_op jit(solution)/shard_map/ppermute | solution.py:365
  59.8 1.6 %collective-permute-start.31 = (f32[2,32,8,128]{3,2,1,0:T(8,128)S(1)}, f32[2,32,8,128]{3,2,1,0:T(8,128)S(1)}, u32[]{:S(2)}, u32[]{:S(2)}) collective-permute-start(f32[2,32,8,128]{3,2,1,0:T(8,128)S(1)} %get-tuple-element.174), channel_id=1, source_target_pairs={{0,4},{4,0},{1,5},{5,1},{2,6},{6,2},{3,7},{7,3},{8,12},{12,8},{9,1... | collective-permute-start | bytes 786440 | tf_op jit(solution)/shard_map/ppermute | solution.py:365
  62.7 2.0 %collective-permute-start.29 = (f32[2,32,8,128]{3,2,1,0:T(8,128)S(1)}, f32[2,32,8,128]{3,2,1,0:T(8,128)S(1)}, u32[]{:S(2)}, u32[]{:S(2)}) collective-permute-start(f32[2,32,8,128]{3,2,1,0:T(8,128)S(1)} %get-tuple-element.169), channel_id=1, source_target_pairs={{0,4},{4,0},{1,5},{5,1},{2,6},{6,2},{3,7},{7,3},{8,12},{12,8},{9,1... | collective-permute-start | bytes 786440 | tf_op jit(solution)/shard_map/ppermute | solution.py:365
  65.3 1.6 %collective-permute-start.33 = (f32[2,32,8,128]{3,2,1,0:T(8,128)S(1)}, f32[2,32,8,128]{3,2,1,0:T(8,128)S(1)}, u32[]{:S(2)}, u32[]{:S(2)}) collective-permute-start(f32[2,32,8,128]{3,2,1,0:T(8,128)S(1)} %get-tuple-element.178), channel_id=1, source_target_pairs={{0,8},{8,0},{1,9},{9,1},{2,10},{10,2},{3,11},{11,3},{4,12},{12,4},... | collective-permute-start | bytes 786440 | tf_op jit(solution)/shard_map/ppermute | solution.py:365
  66.9 1.4 %collective-permute-done.30.refs_4_ = f32[2,32,8,128]{3,2,1,0:T(8,128)S(1)} collective-permute-done((f32[2,32,8,128]{3,2,1,0:T(8,128)S(1)}, f32[2,32,8,128]{3,2,1,0:T(8,128)S(1)}, u32[]{:S(2)}, u32[]{:S(2)}) %collective-permute-start.30) | collective-permute-done | bytes 262176 | tf_op jit(solution)/shard_map/ppermute | solution.py:365
  69.3 1.5 %collective-permute-start.34 = (f32[2,32,8,128]{3,2,1,0:T(8,128)S(1)}, f32[2,32,8,128]{3,2,1,0:T(8,128)S(1)}, u32[]{:S(2)}, u32[]{:S(2)}) collective-permute-start(f32[2,32,8,128]{3,2,1,0:T(8,128)S(1)} %get-tuple-element.179), channel_id=1, source_target_pairs={{0,4},{4,0},{1,5},{5,1},{2,6},{6,2},{3,7},{7,3},{8,12},{12,8},{9,1... | collective-permute-start | bytes 786440 | tf_op jit(solution)/shard_map/ppermute | solution.py:365
  72.5 1.4 %collective-permute-done.28.refs_4_ = f32[2,32,8,128]{3,2,1,0:T(8,128)S(1)} collective-permute-done((f32[2,32,8,128]{3,2,1,0:T(8,128)S(1)}, f32[2,32,8,128]{3,2,1,0:T(8,128)S(1)}, u32[]{:S(2)}, u32[]{:S(2)}) %collective-permute-start.28) | collective-permute-done | bytes 262176 | tf_op jit(solution)/shard_map/ppermute | solution.py:365
  73.9 2.0 %collective-permute-start.39 = (f32[2,32,8,128]{3,2,1,0:T(8,128)S(1)}, f32[2,32,8,128]{3,2,1,0:T(8,128)S(1)}, u32[]{:S(2)}, u32[]{:S(2)}) collective-permute-start(f32[2,32,8,128]{3,2,1,0:T(8,128)S(1)} %get-tuple-element.189), channel_id=1, source_target_pairs={{0,4},{4,0},{1,5},{5,1},{2,6},{6,2},{3,7},{7,3},{8,12},{12,8},{9,1... | collective-permute-start | bytes 786440 | tf_op jit(solution)/shard_map/ppermute | solution.py:365
  76.6 1.2 %collective-permute-done.32.refs_2_ = f32[8,8,128]{2,1,0:T(8,128)S(1)} collective-permute-done((f32[8,8,128]{2,1,0:T(8,128)S(1)}, f32[8,8,128]{2,1,0:T(8,128)S(1)}, u32[]{:S(2)}, u32[]{:S(2)}) %collective-permute-start.32) | collective-permute-done | bytes 32800 | tf_op jit(solution)/shard_map/ppermute | solution.py:381
  77.8 1.5 %collective-permute-start.36 = (f32[2,32,8,128]{3,2,1,0:T(8,128)S(1)}, f32[2,32,8,128]{3,2,1,0:T(8,128)S(1)}, u32[]{:S(2)}, u32[]{:S(2)}) collective-permute-start(f32[2,32,8,128]{3,2,1,0:T(8,128)S(1)} %get-tuple-element.183), channel_id=1, source_target_pairs={{0,8},{8,0},{1,9},{9,1},{2,10},{10,2},{3,11},{11,3},{4,12},{12,4},... | collective-permute-start | bytes 786440 | tf_op jit(solution)/shard_map/ppermute | solution.py:365
  79.5 2.0 %collective-permute-start.37 = (f32[2,32,8,128]{3,2,1,0:T(8,128)S(1)}, f32[2,32,8,128]{3,2,1,0:T(8,128)S(1)}, u32[]{:S(2)}, u32[]{:S(2)}) collective-permute-start(f32[2,32,8,128]{3,2,1,0:T(8,128)S(1)} %get-tuple-element.184), channel_id=1, source_target_pairs={{0,4},{4,0},{1,5},{5,1},{2,6},{6,2},{3,7},{7,3},{8,12},{12,8},{9,1... | collective-permute-start | bytes 786440 | tf_op jit(solution)/shard_map/ppermute | solution.py:365
  82.1 3.0 %collective-permute-done.38.refs_4_ = f32[2,32,8,128]{3,2,1,0:T(8,128)S(1)} collective-permute-done((f32[2,32,8,128]{3,2,1,0:T(8,128)S(1)}, f32[2,32,8,128]{3,2,1,0:T(8,128)S(1)}, u32[]{:S(2)}, u32[]{:S(2)}) %collective-permute-start.38) | collective-permute-done | bytes 262176 | tf_op jit(solution)/shard_map/ppermute | solution.py:365
  87.9 1.5 %collective-permute-start.49 = (f32[2,32,4,128]{3,2,1,0:T(4,128)S(1)}, f32[2,32,4,128]{3,2,1,0:T(4,128)S(1)}, u32[]{:S(2)}, u32[]{:S(2)}) collective-permute-start(f32[2,32,4,128]{3,2,1,0:T(4,128)S(1)} %get-tuple-element.214), channel_id=1, source_target_pairs={{0,4},{4,0},{1,5},{5,1},{2,6},{6,2},{3,7},{7,3},{8,12},{12,8},{9,1... | collective-permute-start | bytes 393224 | tf_op jit(solution)/shard_map/ppermute | solution.py:365
  89.3 1.2 %collective-permute-done.35.refs_3_ = f32[8,8,128]{2,1,0:T(8,128)S(1)} collective-permute-done((f32[8,8,128]{2,1,0:T(8,128)S(1)}, f32[8,8,128]{2,1,0:T(8,128)S(1)}, u32[]{:S(2)}, u32[]{:S(2)}) %collective-permute-start.35) | collective-permute-done | bytes 32800 | tf_op jit(solution)/shard_map/ppermute | solution.py:382
  90.8 2.0 %collective-permute-start.46 = (f32[32,8,128]{2,1,0:T(8,128)S(1)}, f32[32,8,128]{2,1,0:T(8,128)S(1)}, u32[]{:S(2)}, u32[]{:S(2)}) collective-permute-start(f32[32,8,128]{2,1,0:T(8,128)S(1)} %get-tuple-element.210), channel_id=1, source_target_pairs={{0,8},{8,0},{1,9},{9,1},{2,10},{10,2},{3,11},{11,3},{4,12},{12,4},... | collective-permute-start | bytes 393224 | tf_op jit(solution)/shard_map/ppermute | solution.py:410
  94.7 1.5 %collective-permute-start.42 = (f32[2,64,4,128]{3,2,1,0:T(4,128)S(1)}, f32[2,64,4,128]{3,2,1,0:T(4,128)S(1)}, u32[]{:S(2)}, u32[]{:S(2)}) collective-permute-start(f32[2,64,4,128]{3,2,1,0:T(4,128)S(1)} %get-tuple-element.198), channel_id=1, source_target_pairs={{0,4},{4,0},{1,5},{5,1},{2,6},{6,2},{3,7},{7,3},{8,12},{12,8},{9,1... | collective-permute-start | bytes 786440 | tf_op jit(solution)/shard_map/ppermute | solution.py:365
  97.7 1.5 %collective-permute-start.51 = (f32[2,32,4,128]{3,2,1,0:T(4,128)S(1)}, f32[2,32,4,128]{3,2,1,0:T(4,128)S(1)}, u32[]{:S(2)}, u32[]{:S(2)}) collective-permute-start(f32[2,32,4,128]{3,2,1,0:T(4,128)S(1)} %get-tuple-element.218), channel_id=1, source_target_pairs={{0,4},{4,0},{1,5},{5,1},{2,6},{6,2},{3,7},{7,3},{8,12},{12,8},{9,1... | collective-permute-start | bytes 393224 | tf_op jit(solution)/shard_map/ppermute | solution.py:365
  99.2 7.5 %collective-permute-done.47.refs_5_ = f32[2,32,4,128]{3,2,1,0:T(4,128)S(1)} collective-permute-done((f32[2,32,4,128]{3,2,1,0:T(4,128)S(1)}, f32[2,32,4,128]{3,2,1,0:T(4,128)S(1)}, u32[]{:S(2)}, u32[]{:S(2)}) %collective-permute-start.47) | collective-permute-done | bytes 131104 | tf_op jit(solution)/shard_map/ppermute | solution.py:365
  107.6 1.5 %collective-permute-start.45 = (f32[2,32,4,128]{3,2,1,0:T(4,128)S(1)}, f32[2,32,4,128]{3,2,1,0:T(4,128)S(1)}, u32[]{:S(2)}, u32[]{:S(2)}) collective-permute-start(f32[2,32,4,128]{3,2,1,0:T(4,128)S(1)} %get-tuple-element.208), channel_id=1, source_target_pairs={{0,4},{4,0},{1,5},{5,1},{2,6},{6,2},{3,7},{7,3},{8,12},{12,8},{9,1... | collective-permute-start | bytes 393224 | tf_op jit(solution)/shard_map/ppermute | solution.py:365
  111.6 1.7 %close.2 = (f32[96,8,8,128]{3,2,1,0:T(8,128)}, f32[96,8,8,128]{3,2,1,0:T(8,128)}) custom-call(f32[32,4,8,128]{3,2,1,0:T(8,128)S(1)} %get-tuple-element.212.refs_0_, f32[32,4,8,128]{3,2,1,0:T(8,128)S(1)} %get-tuple-element.216.refs_1_, f32[32,4,8,128]{3,2,1,0:T(8,128)S(1)} %get-tuple-element.220.refs_2_, f32[2,4,8,128]{3,2,1,0:T(8,128)S(1)} %get-tuple-element.221.refs_3_, ...), custom_call_target="tpu_custom_call" | custom-call | flops 1179648 | bytes 6291456 | tf_op jit(solution)/shard_map/close/pallas_call | solution.py:343
  115.9 1.2 %close.3 = f32[96,8,8,128]{3,2,1,0:T(8,128)} custom-call(f32[32,4,8,128]{3,2,1,0:T(8,128)S(1)} %get-tuple-element.199.refs_0_, f32[32,4,8,128]{3,2,1,0:T(8,128)S(1)} %get-tuple-element.204.refs_1_, f32[32,4,8,128]{3,2,1,0:T(8,128)S(1)} %get-tuple-element.223.refs_2_, ...), custom_call_target="tpu_custom_call", output_to_operand_aliasing={{}: (5, {})} | custom-call | flops 1179648 | bytes 6291456 | tf_op jit(solution)/shard_map/close/pallas_call | solution.py:343
  (89 shorter events, 31.0 us)
Async XLA Ops:
  1.9 11.1 %collective-permute-start.1 = (f32[2,32,8,128]{3,2,1,0:T(8,128)S(1)}, f32[2,32,8,128]{3,2,1,0:T(8,128)S(1)}, u32[]{:S(2)}, u32[]{:S(2)}) collective-permute-start(f32[2,32,8,128]{3,2,1,0:T(8,128)S(1)} %get-tuple-element.118), channel_id=1, source_target_pairs={{0,8},{8,0},{1,9},{9,1},{2,10},{10,2},{3,11},{11,3},{4,12},{12,4},... | collective-permute-start | bytes 786440 | tf_op jit(solution)/shard_map/ppermute | solution.py:365
  5.0 9.6 %collective-permute-start.2 = (f32[2,32,8,128]{3,2,1,0:T(8,128)S(1)}, f32[2,32,8,128]{3,2,1,0:T(8,128)S(1)}, u32[]{:S(2)}, u32[]{:S(2)}) collective-permute-start(f32[2,32,8,128]{3,2,1,0:T(8,128)S(1)} %get-tuple-element.119), channel_id=1, source_target_pairs={{0,4},{4,0},{1,5},{5,1},{2,6},{6,2},{3,7},{7,3},{8,12},{12,8},{9,1... | collective-permute-start | bytes 786440 | tf_op jit(solution)/shard_map/ppermute | solution.py:365
  7.9 9.9 %collective-permute-start.6 = (f32[2,32,8,128]{3,2,1,0:T(8,128)S(1)}, f32[2,32,8,128]{3,2,1,0:T(8,128)S(1)}, u32[]{:S(2)}, u32[]{:S(2)}) collective-permute-start(f32[2,32,8,128]{3,2,1,0:T(8,128)S(1)} %get-tuple-element.128), channel_id=1, source_target_pairs={{0,8},{8,0},{1,9},{9,1},{2,10},{10,2},{3,11},{11,3},{4,12},{12,4},... | collective-permute-start | bytes 786440 | tf_op jit(solution)/shard_map/ppermute | solution.py:365
  8.5 11.3 %collective-permute-start.7 = (f32[2,32,8,128]{3,2,1,0:T(8,128)S(1)}, f32[2,32,8,128]{3,2,1,0:T(8,128)S(1)}, u32[]{:S(2)}, u32[]{:S(2)}) collective-permute-start(f32[2,32,8,128]{3,2,1,0:T(8,128)S(1)} %get-tuple-element.129), channel_id=1, source_target_pairs={{0,4},{4,0},{1,5},{5,1},{2,6},{6,2},{3,7},{7,3},{8,12},{12,8},{9,1... | collective-permute-start | bytes 786440 | tf_op jit(solution)/shard_map/ppermute | solution.py:365
  9.8 1.3 %collective-permute-start = (f32[8,8,128]{2,1,0:T(8,128)S(1)}, f32[8,8,128]{2,1,0:T(8,128)S(1)}, u32[]{:S(2)}, u32[]{:S(2)}) collective-permute-start(f32[8,8,128]{2,1,0:T(8,128)S(1)} %get-tuple-element.117), channel_id=1, source_target_pairs={{0,16},{16,0},{1,17},{17,1},{2,18},{18,2},{3,19},{19,3},{4,20},{20... | collective-permute-start | bytes 98312 | tf_op jit(solution)/shard_map/ppermute | solution.py:381
  11.1 12.3 %collective-permute-start.4 = (f32[2,32,8,128]{3,2,1,0:T(8,128)S(1)}, f32[2,32,8,128]{3,2,1,0:T(8,128)S(1)}, u32[]{:S(2)}, u32[]{:S(2)}) collective-permute-start(f32[2,32,8,128]{3,2,1,0:T(8,128)S(1)} %get-tuple-element.123), channel_id=1, source_target_pairs={{0,8},{8,0},{1,9},{9,1},{2,10},{10,2},{3,11},{11,3},{4,12},{12,4},... | collective-permute-start | bytes 786440 | tf_op jit(solution)/shard_map/ppermute | solution.py:365
  13.1 12.3 %collective-permute-start.5 = (f32[2,32,8,128]{3,2,1,0:T(8,128)S(1)}, f32[2,32,8,128]{3,2,1,0:T(8,128)S(1)}, u32[]{:S(2)}, u32[]{:S(2)}) collective-permute-start(f32[2,32,8,128]{3,2,1,0:T(8,128)S(1)} %get-tuple-element.124), channel_id=1, source_target_pairs={{0,4},{4,0},{1,5},{5,1},{2,6},{6,2},{3,7},{7,3},{8,12},{12,8},{9,1... | collective-permute-start | bytes 786440 | tf_op jit(solution)/shard_map/ppermute | solution.py:365
  15.2 13.8 %collective-permute-start.9 = (f32[2,32,8,128]{3,2,1,0:T(8,128)S(1)}, f32[2,32,8,128]{3,2,1,0:T(8,128)S(1)}, u32[]{:S(2)}, u32[]{:S(2)}) collective-permute-start(f32[2,32,8,128]{3,2,1,0:T(8,128)S(1)} %get-tuple-element.133), channel_id=1, source_target_pairs={{0,8},{8,0},{1,9},{9,1},{2,10},{10,2},{3,11},{11,3},{4,12},{12,4},... | collective-permute-start | bytes 786440 | tf_op jit(solution)/shard_map/ppermute | solution.py:365
  17.7 13.3 %collective-permute-start.10 = (f32[2,32,8,128]{3,2,1,0:T(8,128)S(1)}, f32[2,32,8,128]{3,2,1,0:T(8,128)S(1)}, u32[]{:S(2)}, u32[]{:S(2)}) collective-permute-start(f32[2,32,8,128]{3,2,1,0:T(8,128)S(1)} %get-tuple-element.134), channel_id=1, source_target_pairs={{0,4},{4,0},{1,5},{5,1},{2,6},{6,2},{3,7},{7,3},{8,12},{12,8},{9,1... | collective-permute-start | bytes 786440 | tf_op jit(solution)/shard_map/ppermute | solution.py:365
  21.0 13.6 %collective-permute-start.14 = (f32[2,32,8,128]{3,2,1,0:T(8,128)S(1)}, f32[2,32,8,128]{3,2,1,0:T(8,128)S(1)}, u32[]{:S(2)}, u32[]{:S(2)}) collective-permute-start(f32[2,32,8,128]{3,2,1,0:T(8,128)S(1)} %get-tuple-element.143), channel_id=1, source_target_pairs={{0,8},{8,0},{1,9},{9,1},{2,10},{10,2},{3,11},{11,3},{4,12},{12,4},... | collective-permute-start | bytes 786440 | tf_op jit(solution)/shard_map/ppermute | solution.py:365
  23.4 13.3 %collective-permute-start.15 = (f32[2,32,8,128]{3,2,1,0:T(8,128)S(1)}, f32[2,32,8,128]{3,2,1,0:T(8,128)S(1)}, u32[]{:S(2)}, u32[]{:S(2)}) collective-permute-start(f32[2,32,8,128]{3,2,1,0:T(8,128)S(1)} %get-tuple-element.144), channel_id=1, source_target_pairs={{0,4},{4,0},{1,5},{5,1},{2,6},{6,2},{3,7},{7,3},{8,12},{12,8},{9,1... | collective-permute-start | bytes 786440 | tf_op jit(solution)/shard_map/ppermute | solution.py:365
  26.0 1.3 %collective-permute-start.8 = (f32[8,8,128]{2,1,0:T(8,128)S(1)}, f32[8,8,128]{2,1,0:T(8,128)S(1)}, u32[]{:S(2)}, u32[]{:S(2)}) collective-permute-start(f32[8,8,128]{2,1,0:T(8,128)S(1)} %get-tuple-element.132), channel_id=1, source_target_pairs={{0,16},{16,0},{1,17},{17,1},{2,18},{18,2},{3,19},{19,3},{4,20},{20... | collective-permute-start | bytes 98312 | tf_op jit(solution)/shard_map/ppermute | solution.py:381
  27.3 12.9 %collective-permute-start.12 = (f32[2,32,8,128]{3,2,1,0:T(8,128)S(1)}, f32[2,32,8,128]{3,2,1,0:T(8,128)S(1)}, u32[]{:S(2)}, u32[]{:S(2)}) collective-permute-start(f32[2,32,8,128]{3,2,1,0:T(8,128)S(1)} %get-tuple-element.138), channel_id=1, source_target_pairs={{0,8},{8,0},{1,9},{9,1},{2,10},{10,2},{3,11},{11,3},{4,12},{12,4},... | collective-permute-start | bytes 786440 | tf_op jit(solution)/shard_map/ppermute | solution.py:365
  29.0 13.3 %collective-permute-start.13 = (f32[2,32,8,128]{3,2,1,0:T(8,128)S(1)}, f32[2,32,8,128]{3,2,1,0:T(8,128)S(1)}, u32[]{:S(2)}, u32[]{:S(2)}) collective-permute-start(f32[2,32,8,128]{3,2,1,0:T(8,128)S(1)} %get-tuple-element.139), channel_id=1, source_target_pairs={{0,4},{4,0},{1,5},{5,1},{2,6},{6,2},{3,7},{7,3},{8,12},{12,8},{9,1... | collective-permute-start | bytes 786440 | tf_op jit(solution)/shard_map/ppermute | solution.py:365
  31.6 14.2 %collective-permute-start.17 = (f32[2,32,8,128]{3,2,1,0:T(8,128)S(1)}, f32[2,32,8,128]{3,2,1,0:T(8,128)S(1)}, u32[]{:S(2)}, u32[]{:S(2)}) collective-permute-start(f32[2,32,8,128]{3,2,1,0:T(8,128)S(1)} %get-tuple-element.148), channel_id=1, source_target_pairs={{0,8},{8,0},{1,9},{9,1},{2,10},{10,2},{3,11},{11,3},{4,12},{12,4},... | collective-permute-start | bytes 786440 | tf_op jit(solution)/shard_map/ppermute | solution.py:365
  34.6 13.3 %collective-permute-start.18 = (f32[2,32,8,128]{3,2,1,0:T(8,128)S(1)}, f32[2,32,8,128]{3,2,1,0:T(8,128)S(1)}, u32[]{:S(2)}, u32[]{:S(2)}) collective-permute-start(f32[2,32,8,128]{3,2,1,0:T(8,128)S(1)} %get-tuple-element.149), channel_id=1, source_target_pairs={{0,4},{4,0},{1,5},{5,1},{2,6},{6,2},{3,7},{7,3},{8,12},{12,8},{9,1... | collective-permute-start | bytes 786440 | tf_op jit(solution)/shard_map/ppermute | solution.py:365
  37.8 13.6 %collective-permute-start.22 = (f32[2,32,8,128]{3,2,1,0:T(8,128)S(1)}, f32[2,32,8,128]{3,2,1,0:T(8,128)S(1)}, u32[]{:S(2)}, u32[]{:S(2)}) collective-permute-start(f32[2,32,8,128]{3,2,1,0:T(8,128)S(1)} %get-tuple-element.158), channel_id=1, source_target_pairs={{0,8},{8,0},{1,9},{9,1},{2,10},{10,2},{3,11},{11,3},{4,12},{12,4},... | collective-permute-start | bytes 786440 | tf_op jit(solution)/shard_map/ppermute | solution.py:365
  40.2 13.3 %collective-permute-start.23 = (f32[2,32,8,128]{3,2,1,0:T(8,128)S(1)}, f32[2,32,8,128]{3,2,1,0:T(8,128)S(1)}, u32[]{:S(2)}, u32[]{:S(2)}) collective-permute-start(f32[2,32,8,128]{3,2,1,0:T(8,128)S(1)} %get-tuple-element.159), channel_id=1, source_target_pairs={{0,4},{4,0},{1,5},{5,1},{2,6},{6,2},{3,7},{7,3},{8,12},{12,8},{9,1... | collective-permute-start | bytes 786440 | tf_op jit(solution)/shard_map/ppermute | solution.py:365
  42.8 1.3 %collective-permute-start.16 = (f32[8,8,128]{2,1,0:T(8,128)S(1)}, f32[8,8,128]{2,1,0:T(8,128)S(1)}, u32[]{:S(2)}, u32[]{:S(2)}) collective-permute-start(f32[8,8,128]{2,1,0:T(8,128)S(1)} %get-tuple-element.147), channel_id=1, source_target_pairs={{0,16},{16,0},{1,17},{17,1},{2,18},{18,2},{3,19},{19,3},{4,20},{20... | collective-permute-start | bytes 98312 | tf_op jit(solution)/shard_map/ppermute | solution.py:381
  44.1 12.9 %collective-permute-start.20 = (f32[2,32,8,128]{3,2,1,0:T(8,128)S(1)}, f32[2,32,8,128]{3,2,1,0:T(8,128)S(1)}, u32[]{:S(2)}, u32[]{:S(2)}) collective-permute-start(f32[2,32,8,128]{3,2,1,0:T(8,128)S(1)} %get-tuple-element.153), channel_id=1, source_target_pairs={{0,8},{8,0},{1,9},{9,1},{2,10},{10,2},{3,11},{11,3},{4,12},{12,4},... | collective-permute-start | bytes 786440 | tf_op jit(solution)/shard_map/ppermute | solution.py:365
  45.8 13.3 %collective-permute-start.21 = (f32[2,32,8,128]{3,2,1,0:T(8,128)S(1)}, f32[2,32,8,128]{3,2,1,0:T(8,128)S(1)}, u32[]{:S(2)}, u32[]{:S(2)}) collective-permute-start(f32[2,32,8,128]{3,2,1,0:T(8,128)S(1)} %get-tuple-element.154), channel_id=1, source_target_pairs={{0,4},{4,0},{1,5},{5,1},{2,6},{6,2},{3,7},{7,3},{8,12},{12,8},{9,1... | collective-permute-start | bytes 786440 | tf_op jit(solution)/shard_map/ppermute | solution.py:365
  48.5 14.2 %collective-permute-start.25 = (f32[2,32,8,128]{3,2,1,0:T(8,128)S(1)}, f32[2,32,8,128]{3,2,1,0:T(8,128)S(1)}, u32[]{:S(2)}, u32[]{:S(2)}) collective-permute-start(f32[2,32,8,128]{3,2,1,0:T(8,128)S(1)} %get-tuple-element.163), channel_id=1, source_target_pairs={{0,8},{8,0},{1,9},{9,1},{2,10},{10,2},{3,11},{11,3},{4,12},{12,4},... | collective-permute-start | bytes 786440 | tf_op jit(solution)/shard_map/ppermute | solution.py:365
  51.4 13.2 %collective-permute-start.26 = (f32[2,32,8,128]{3,2,1,0:T(8,128)S(1)}, f32[2,32,8,128]{3,2,1,0:T(8,128)S(1)}, u32[]{:S(2)}, u32[]{:S(2)}) collective-permute-start(f32[2,32,8,128]{3,2,1,0:T(8,128)S(1)} %get-tuple-element.164), channel_id=1, source_target_pairs={{0,4},{4,0},{1,5},{5,1},{2,6},{6,2},{3,7},{7,3},{8,12},{12,8},{9,1... | collective-permute-start | bytes 786440 | tf_op jit(solution)/shard_map/ppermute | solution.py:365
  54.7 13.6 %collective-permute-start.30 = (f32[2,32,8,128]{3,2,1,0:T(8,128)S(1)}, f32[2,32,8,128]{3,2,1,0:T(8,128)S(1)}, u32[]{:S(2)}, u32[]{:S(2)}) collective-permute-start(f32[2,32,8,128]{3,2,1,0:T(8,128)S(1)} %get-tuple-element.173), channel_id=1, source_target_pairs={{0,8},{8,0},{1,9},{9,1},{2,10},{10,2},{3,11},{11,3},{4,12},{12,4},... | collective-permute-start | bytes 786440 | tf_op jit(solution)/shard_map/ppermute | solution.py:365
  59.7 1.6 %collective-permute-start.24 = (f32[8,8,128]{2,1,0:T(8,128)S(1)}, f32[8,8,128]{2,1,0:T(8,128)S(1)}, u32[]{:S(2)}, u32[]{:S(2)}) collective-permute-start(f32[8,8,128]{2,1,0:T(8,128)S(1)} %get-tuple-element.162), channel_id=1, source_target_pairs={{0,16},{16,0},{1,17},{17,1},{2,18},{18,2},{3,19},{19,3},{4,20},{20... | collective-permute-start | bytes 98312 | tf_op jit(solution)/shard_map/ppermute | solution.py:381
  59.8 9.6 %collective-permute-start.31 = (f32[2,32,8,128]{3,2,1,0:T(8,128)S(1)}, f32[2,32,8,128]{3,2,1,0:T(8,128)S(1)}, u32[]{:S(2)}, u32[]{:S(2)}) collective-permute-start(f32[2,32,8,128]{3,2,1,0:T(8,128)S(1)} %get-tuple-element.174), channel_id=1, source_target_pairs={{0,4},{4,0},{1,5},{5,1},{2,6},{6,2},{3,7},{7,3},{8,12},{12,8},{9,1... | collective-permute-start | bytes 786440 | tf_op jit(solution)/shard_map/ppermute | solution.py:365
  61.3 12.6 %collective-permute-start.28 = (f32[2,32,8,128]{3,2,1,0:T(8,128)S(1)}, f32[2,32,8,128]{3,2,1,0:T(8,128)S(1)}, u32[]{:S(2)}, u32[]{:S(2)}) collective-permute-start(f32[2,32,8,128]{3,2,1,0:T(8,128)S(1)} %get-tuple-element.168), channel_id=1, source_target_pairs={{0,8},{8,0},{1,9},{9,1},{2,10},{10,2},{3,11},{11,3},{4,12},{12,4},... | collective-permute-start | bytes 786440 | tf_op jit(solution)/shard_map/ppermute | solution.py:365
  62.7 13.2 %collective-permute-start.29 = (f32[2,32,8,128]{3,2,1,0:T(8,128)S(1)}, f32[2,32,8,128]{3,2,1,0:T(8,128)S(1)}, u32[]{:S(2)}, u32[]{:S(2)}) collective-permute-start(f32[2,32,8,128]{3,2,1,0:T(8,128)S(1)} %get-tuple-element.169), channel_id=1, source_target_pairs={{0,4},{4,0},{1,5},{5,1},{2,6},{6,2},{3,7},{7,3},{8,12},{12,8},{9,1... | collective-permute-start | bytes 786440 | tf_op jit(solution)/shard_map/ppermute | solution.py:365
  65.3 14.2 %collective-permute-start.33 = (f32[2,32,8,128]{3,2,1,0:T(8,128)S(1)}, f32[2,32,8,128]{3,2,1,0:T(8,128)S(1)}, u32[]{:S(2)}, u32[]{:S(2)}) collective-permute-start(f32[2,32,8,128]{3,2,1,0:T(8,128)S(1)} %get-tuple-element.178), channel_id=1, source_target_pairs={{0,8},{8,0},{1,9},{9,1},{2,10},{10,2},{3,11},{11,3},{4,12},{12,4},... | collective-permute-start | bytes 786440 | tf_op jit(solution)/shard_map/ppermute | solution.py:365
  68.3 3.1 %collective-permute-start.27 = (f32[8,8,128]{2,1,0:T(8,128)S(1)}, f32[8,8,128]{2,1,0:T(8,128)S(1)}, u32[]{:S(2)}, u32[]{:S(2)}) collective-permute-start(f32[8,8,128]{2,1,0:T(8,128)S(1)} %get-tuple-element.160.refs_6_), channel_id=1, source_target_pairs={{16,0},{0,16},{17,1},{1,17},{18,2},{2,18},{19,3},{3,19},{20,4},{4,... | collective-permute-start | bytes 98312 | tf_op jit(solution)/shard_map/ppermute | solution.py:382
  69.3 12.2 %collective-permute-start.34 = (f32[2,32,8,128]{3,2,1,0:T(8,128)S(1)}, f32[2,32,8,128]{3,2,1,0:T(8,128)S(1)}, u32[]{:S(2)}, u32[]{:S(2)}) collective-permute-start(f32[2,32,8,128]{3,2,1,0:T(8,128)S(1)} %get-tuple-element.179), channel_id=1, source_target_pairs={{0,4},{4,0},{1,5},{5,1},{2,6},{6,2},{3,7},{7,3},{8,12},{12,8},{9,1... | collective-permute-start | bytes 786440 | tf_op jit(solution)/shard_map/ppermute | solution.py:365
  71.4 13.7 %collective-permute-start.38 = (f32[2,32,8,128]{3,2,1,0:T(8,128)S(1)}, f32[2,32,8,128]{3,2,1,0:T(8,128)S(1)}, u32[]{:S(2)}, u32[]{:S(2)}) collective-permute-start(f32[2,32,8,128]{3,2,1,0:T(8,128)S(1)} %get-tuple-element.188), channel_id=1, source_target_pairs={{0,8},{8,0},{1,9},{9,1},{2,10},{10,2},{3,11},{11,3},{4,12},{12,4},... | collective-permute-start | bytes 786440 | tf_op jit(solution)/shard_map/ppermute | solution.py:365
  73.9 12.3 %collective-permute-start.39 = (f32[2,32,8,128]{3,2,1,0:T(8,128)S(1)}, f32[2,32,8,128]{3,2,1,0:T(8,128)S(1)}, u32[]{:S(2)}, u32[]{:S(2)}) collective-permute-start(f32[2,32,8,128]{3,2,1,0:T(8,128)S(1)} %get-tuple-element.189), channel_id=1, source_target_pairs={{0,4},{4,0},{1,5},{5,1},{2,6},{6,2},{3,7},{7,3},{8,12},{12,8},{9,1... | collective-permute-start | bytes 786440 | tf_op jit(solution)/shard_map/ppermute | solution.py:365
  76.5 1.3 %collective-permute-start.32 = (f32[8,8,128]{2,1,0:T(8,128)S(1)}, f32[8,8,128]{2,1,0:T(8,128)S(1)}, u32[]{:S(2)}, u32[]{:S(2)}) collective-permute-start(f32[8,8,128]{2,1,0:T(8,128)S(1)} %get-tuple-element.177), channel_id=1, source_target_pairs={{0,16},{16,0},{1,17},{17,1},{2,18},{18,2},{3,19},{19,3},{4,20},{20... | collective-permute-start | bytes 98312 | tf_op jit(solution)/shard_map/ppermute | solution.py:381
  77.8 13.0 %collective-permute-start.36 = (f32[2,32,8,128]{3,2,1,0:T(8,128)S(1)}, f32[2,32,8,128]{3,2,1,0:T(8,128)S(1)}, u32[]{:S(2)}, u32[]{:S(2)}) collective-permute-start(f32[2,32,8,128]{3,2,1,0:T(8,128)S(1)} %get-tuple-element.183), channel_id=1, source_target_pairs={{0,8},{8,0},{1,9},{9,1},{2,10},{10,2},{3,11},{11,3},{4,12},{12,4},... | collective-permute-start | bytes 786440 | tf_op jit(solution)/shard_map/ppermute | solution.py:365
  79.5 13.3 %collective-permute-start.37 = (f32[2,32,8,128]{3,2,1,0:T(8,128)S(1)}, f32[2,32,8,128]{3,2,1,0:T(8,128)S(1)}, u32[]{:S(2)}, u32[]{:S(2)}) collective-permute-start(f32[2,32,8,128]{3,2,1,0:T(8,128)S(1)} %get-tuple-element.184), channel_id=1, source_target_pairs={{0,4},{4,0},{1,5},{5,1},{2,6},{6,2},{3,7},{7,3},{8,12},{12,8},{9,1... | collective-permute-start | bytes 786440 | tf_op jit(solution)/shard_map/ppermute | solution.py:365
  86.8 9.4 %collective-permute-start.48 = (f32[32,8,128]{2,1,0:T(8,128)S(1)}, f32[32,8,128]{2,1,0:T(8,128)S(1)}, u32[]{:S(2)}, u32[]{:S(2)}) collective-permute-start(f32[32,8,128]{2,1,0:T(8,128)S(1)} %get-tuple-element.213), channel_id=1, source_target_pairs={{0,8},{8,0},{1,9},{9,1},{2,10},{10,2},{3,11},{11,3},{4,12},{12,4},... | collective-permute-start | bytes 393224 | tf_op jit(solution)/shard_map/ppermute | solution.py:410
  87.9 8.9 %collective-permute-start.49 = (f32[2,32,4,128]{3,2,1,0:T(4,128)S(1)}, f32[2,32,4,128]{3,2,1,0:T(4,128)S(1)}, u32[]{:S(2)}, u32[]{:S(2)}) collective-permute-start(f32[2,32,4,128]{3,2,1,0:T(4,128)S(1)} %get-tuple-element.214), channel_id=1, source_target_pairs={{0,4},{4,0},{1,5},{5,1},{2,6},{6,2},{3,7},{7,3},{8,12},{12,8},{9,1... | collective-permute-start | bytes 393224 | tf_op jit(solution)/shard_map/ppermute | solution.py:365
  90.6 3.0 %collective-permute-start.43 = (f32[8,8,128]{2,1,0:T(8,128)S(1)}, f32[8,8,128]{2,1,0:T(8,128)S(1)}, u32[]{:S(2)}, u32[]{:S(2)}) collective-permute-start(f32[8,8,128]{2,1,0:T(8,128)S(1)} %get-tuple-element.190.refs_6_), channel_id=1, source_target_pairs={{16,0},{0,16},{17,1},{1,17},{18,2},{2,18},{19,3},{3,19},{20,4},{4,... | collective-permute-start | bytes 98312 | tf_op jit(solution)/shard_map/ppermute | solution.py:393
  90.8 6.9 %collective-permute-start.46 = (f32[32,8,128]{2,1,0:T(8,128)S(1)}, f32[32,8,128]{2,1,0:T(8,128)S(1)}, u32[]{:S(2)}, u32[]{:S(2)}) collective-permute-start(f32[32,8,128]{2,1,0:T(8,128)S(1)} %get-tuple-element.210), channel_id=1, source_target_pairs={{0,8},{8,0},{1,9},{9,1},{2,10},{10,2},{3,11},{11,3},{4,12},{12,4},... | collective-permute-start | bytes 393224 | tf_op jit(solution)/shard_map/ppermute | solution.py:410
  93.5 19.8 %collective-permute-start.41 = (f32[64,8,128]{2,1,0:T(8,128)S(1)}, f32[64,8,128]{2,1,0:T(8,128)S(1)}, u32[]{:S(2)}, u32[]{:S(2)}) collective-permute-start(f32[64,8,128]{2,1,0:T(8,128)S(1)} %get-tuple-element.197), channel_id=1, source_target_pairs={{8,0},{0,8},{9,1},{1,9},{10,2},{2,10},{11,3},{3,11},{12,4},{4,12},... | collective-permute-start | bytes 786440 | tf_op jit(solution)/shard_map/ppermute | solution.py:410
  94.7 18.6 %collective-permute-start.42 = (f32[2,64,4,128]{3,2,1,0:T(4,128)S(1)}, f32[2,64,4,128]{3,2,1,0:T(4,128)S(1)}, u32[]{:S(2)}, u32[]{:S(2)}) collective-permute-start(f32[2,64,4,128]{3,2,1,0:T(4,128)S(1)} %get-tuple-element.198), channel_id=1, source_target_pairs={{0,4},{4,0},{1,5},{5,1},{2,6},{6,2},{3,7},{7,3},{8,12},{12,8},{9,1... | collective-permute-start | bytes 786440 | tf_op jit(solution)/shard_map/ppermute | solution.py:365
  96.2 10.5 %collective-permute-start.47 = (f32[2,32,4,128]{3,2,1,0:T(4,128)S(1)}, f32[2,32,4,128]{3,2,1,0:T(4,128)S(1)}, u32[]{:S(2)}, u32[]{:S(2)}) collective-permute-start(f32[2,32,4,128]{3,2,1,0:T(4,128)S(1)} %get-tuple-element.211), channel_id=1, source_target_pairs={{0,4},{4,0},{1,5},{5,1},{2,6},{6,2},{3,7},{7,3},{8,12},{12,8},{9,1... | collective-permute-start | bytes 393224 | tf_op jit(solution)/shard_map/ppermute | solution.py:365
  96.7 10.9 %collective-permute-start.50 = (f32[32,8,128]{2,1,0:T(8,128)S(1)}, f32[32,8,128]{2,1,0:T(8,128)S(1)}, u32[]{:S(2)}, u32[]{:S(2)}) collective-permute-start(f32[32,8,128]{2,1,0:T(8,128)S(1)} %get-tuple-element.217), channel_id=1, source_target_pairs={{0,8},{8,0},{1,9},{9,1},{2,10},{10,2},{3,11},{11,3},{4,12},{12,4},... | collective-permute-start | bytes 393224 | tf_op jit(solution)/shard_map/ppermute | solution.py:410
  97.7 12.2 %collective-permute-start.51 = (f32[2,32,4,128]{3,2,1,0:T(4,128)S(1)}, f32[2,32,4,128]{3,2,1,0:T(4,128)S(1)}, u32[]{:S(2)}, u32[]{:S(2)}) collective-permute-start(f32[2,32,4,128]{3,2,1,0:T(4,128)S(1)} %get-tuple-element.218), channel_id=1, source_target_pairs={{0,4},{4,0},{1,5},{5,1},{2,6},{6,2},{3,7},{7,3},{8,12},{12,8},{9,1... | collective-permute-start | bytes 393224 | tf_op jit(solution)/shard_map/ppermute | solution.py:365
  106.7 7.4 %collective-permute-start.44 = (f32[32,8,128]{2,1,0:T(8,128)S(1)}, f32[32,8,128]{2,1,0:T(8,128)S(1)}, u32[]{:S(2)}, u32[]{:S(2)}) collective-permute-start(f32[32,8,128]{2,1,0:T(8,128)S(1)} %get-tuple-element.207), channel_id=1, source_target_pairs={{8,0},{0,8},{9,1},{1,9},{10,2},{2,10},{11,3},{3,11},{12,4},{4,12},... | collective-permute-start | bytes 393224 | tf_op jit(solution)/shard_map/ppermute | solution.py:410
  107.6 6.5 %collective-permute-start.45 = (f32[2,32,4,128]{3,2,1,0:T(4,128)S(1)}, f32[2,32,4,128]{3,2,1,0:T(4,128)S(1)}, u32[]{:S(2)}, u32[]{:S(2)}) collective-permute-start(f32[2,32,4,128]{3,2,1,0:T(4,128)S(1)} %get-tuple-element.208), channel_id=1, source_target_pairs={{0,4},{4,0},{1,5},{5,1},{2,6},{6,2},{3,7},{7,3},{8,12},{12,8},{9,1... | collective-permute-start | bytes 393224 | tf_op jit(solution)/shard_map/ppermute | solution.py:365
  114.5 1.4 %collective-permute-start.53 = (f32[2,4,8,128]{3,2,1,0:T(8,128)S(1)}, f32[2,4,8,128]{3,2,1,0:T(8,128)S(1)}, u32[]{:S(2)}, u32[]{:S(2)}) collective-permute-start(f32[2,4,8,128]{3,2,1,0:T(8,128)S(1)} %get-tuple-element.224.refs_3_), channel_id=1, source_target_pairs={{0,16},{16,0},{1,17},{17,1},{2,18},{18,2},{3,19},{19,3},{4,20},{20... | collective-permute-start | bytes 98312 | tf_op jit(solution)/shard_map/ppermute | solution.py:407
  (7 other events, 15.5 us)
where the time goes:
time: 117 us
  starting transfers between devices  60.4 us (52%)
  waiting for transfers between devices  36.3 us (31%)
  Pallas kernels  19.6 us (17%)
    ppermute x35, starting transfers between devices, exchange(): return (lax.ppermute(face, axis, up),)  54.5 us
    ppermute x35, waiting for transfers between devices, exchange(): return (lax.ppermute(face, axis, up),)  26.2 us
    pallas_call x15, Pallas kernels, step_chunk(): pl.pallas_call(functools.partial(step_kernel, start, len(x_halo), len(z_h...  9.16 us
    ppermute x6, waiting for transfers between devices, local(): before = lax.ppermute(state[-1][2], 'rows', up)  5.88 us
    ppermute x5, starting transfers between devices, send(): x_halo = lax.ppermute(x_face, 'cols', pairs)  4.97 us
    pallas_call x3, Pallas kernels, open_chunk(): pl.pallas_call(functools.partial(open_kernel, start, parts), out_shape=tu...  3.95 us
    ppermute x6, waiting for transfers between devices, local(): after = lax.ppermute(state[0][1], 'rows', down)  2.98 us
    pallas_call x2, Pallas kernels, close(): pl.pallas_call(functools.partial(close_kernel, starts, span, len(stats) -...  2.96 us
  transfers between devices with their start and end apart: 54, of which 28 were waited for; matrix products, arithmetic and copies ran while one was open for 0% of the time, Pallas kernels for 14%

commit v1 on v0

--- a/solution.py
+++ b/solution.py
@@ -9,7 +9,7 @@
 
 
 STEPS = 6
-CHUNKS = (1, 1, 1)
+CHUNKS = (1, 2, 2, 1)
 EPS = 0.0001
 VMEM_GRANT = 16 << 20
 
@@ -174,7 +174,8 @@
         outs += [vmem_out(rows, zs, levels)] * 2
         outs += [vmem_out(2, rows, cut, levels), vmem_out(2, rows, xs - cut, levels)]
         if gathers:
-            outs += [vmem_out(start, zs, levels), vmem_out(2, start, xs - cut, levels)]
+            before = sum(low.shape[0] for low, _ in held)
+            outs += [vmem_out(before, zs, levels), vmem_out(2, before, xs - cut, levels)]
     else:
         outs += [vmem_out(2, rows, zs, levels), vmem_out(2, rows, xs, levels)]
     return pl.pallas_call(
@@ -376,8 +377,12 @@
     state = []
     for start, rows in pieces:
         state.append(open_chunk(field_values, state[-1][1] if state else field_values, start, rows))
+    gathered = max(chunks - 2, 0)
     for step in range(STEPS - 1):
-        halos = [(exchange(s[3], "cols"), exchange(s[4], "slabs")) for s in state]
+        halos = []
+        for s in state:
+            x_halo = exchange(s[3], "cols")
+            halos.append((x_halo, exchange(s[4], "slabs")))
         before = lax.ppermute(state[-1][2], "rows", up)
         after = lax.ppermute(state[0][1], "rows", down)
         new = []
@@ -385,7 +390,7 @@
             y_before = before if c == 0 else state[c - 1][2]
             y_after = after if c == chunks - 1 else state[c + 1][1]
             halves = step == STEPS - 2
-            held = [(n[3], n[6]) for n in new] if halves and c == chunks - 1 else []
+            held = [(n[3], n[6]) for n in new[:gathered]] if halves and c == chunks - 1 else []
             new.append(step_chunk(s[0], crowding, y_before, y_after, x_halo, z_halo, start,
                                   new[-1][1] if new else s[1], halves, held))
         state = new
@@ -413,10 +418,11 @@
     halos = [send(s[4], x_up, s[5]) for s in state]
     low, low_stats = last_half(low_span, *zip(*halos), [0] * chunks, None)
     scaled, end = close(low, starts, low_span, low_stats, field_values.shape, None)
-    halos = [send(state[-1][3], x_down, state[-1][6])]
-    if chunks > 1:
-        halos = [send(state[-1][7], x_down, state[-1][8])] * (chunks - 1) + halos
-    high, high_stats = last_half(high_span, *zip(*halos), [*starts[:-1], 0], scaled)
+    halos = []
+    if gathered:
+        halos = [send(state[-1][7], x_down, state[-1][8])] * gathered
+    halos += [send(state[c][3], x_down, state[c][6]) for c in range(gathered, chunks)]
+    high, high_stats = last_half(high_span, *zip(*halos), [*starts[:gathered], *[0] * (chunks - gathered)], scaled)
     end = write_parts(high, starts, high_span, end)
     (scaled,) = close(high, starts, high_span, high_stats, field_values.shape, scaled)
     return scaled, end

time: 117 us -> 134 us (1.15)
  waiting for transfers between devices: 36.3 us -> 56.9 us
  starting transfers between devices: 60.4 us -> 55.6 us
    ppermute x35 -> x47, waiting for transfers between devices: 26.2 us -> 47.1 us  [exchange(): return (lax.ppermute(face, axis, up),)]
    ppermute x35 -> x47, starting transfers between devices: 54.5 us -> 48 us  [exchange(): return (lax.ppermute(face, axis, up),)]
    ppermute x5 -> x7, starting transfers between devices: 4.97 us -> 7.04 us  [send(): x_halo = lax.ppermute(x_face, 'cols', pairs)]
    ppermute x5 -> x7, waiting for transfers between devices: 0.01 us -> 1.42 us  [send(): x_halo = lax.ppermute(x_face, 'cols', pairs)]
    pallas_call x3 -> x4, Pallas kernels: 3.95 us -> 4.99 us  [open_chunk(): pl.pallas_call(functools.partial(open_kernel, start, parts), out_shape=tu...]
    pallas_call x15 -> x20, Pallas kernels: 9.16 us -> 9.27 us  [step_chunk(): pl.pallas_call(functools.partial(step_kernel, start, len(x_halo), len(z_h...]
  transfers between devices with their start and end apart: 54 -> 68, of which waited for: 28 -> 23; matrix products, arithmetic and copies ran while one was open for 0% -> 0% of each run, Pallas kernels for 14% -> 14%
where the time goes in v1:
time: 134 us
  waiting for transfers between devices  56.9 us (42%)
  starting transfers between devices  55.6 us (41%)
  Pallas kernels  20.8 us (16%)
    ppermute x47, starting transfers between devices, exchange(): return (lax.ppermute(face, axis, up),)  48 us
    ppermute x47, waiting for transfers between devices, exchange(): return (lax.ppermute(face, axis, up),)  47.1 us
    pallas_call x20, Pallas kernels, step_chunk(): pl.pallas_call(functools.partial(step_kernel, start, len(x_halo), len(z_h...  9.27 us
    ppermute x7, starting transfers between devices, send(): x_halo = lax.ppermute(x_face, 'cols', pairs)  7.04 us
    pallas_call x4, Pallas kernels, open_chunk(): pl.pallas_call(functools.partial(open_kernel, start, parts), out_shape=tu...  4.99 us
    ppermute x6, waiting for transfers between devices, local(): before = lax.ppermute(state[-1][2], 'rows', up)  4.81 us
    pallas_call x2, Pallas kernels, close(): pl.pallas_call(functools.partial(close_kernel, starts, span, len(stats) -...  2.97 us
  transfers between devices with their start and end apart: 68, of which 23 were waited for; matrix products, arithmetic and copies ran while one was open for 0% of the time, Pallas kernels for 14%

profile of v1, /device:TPU:0, one launch (start us, length us, event | category | flops | bytes accessed | tf_op | source)
XLA Modules:
  0.0 134.3 jit_solution(16367062279652903054)
XLA Ops:
  0.6 1.2 open_chunk.4
  1.8 3.1 %collective-permute-start.1 = (f32[2,16,8,128]{3,2,1,0:T(8,128)S(1)}, f32[2,16,8,128]{3,2,1,0:T(8,128)S(1)}, u32[]{:S(2)}, u32[]{:S(2)}) collective-permute-start(f32[2,16,8,128]{3,2,1,0:T(8,128)S(1)} %get-tuple-element.155), channel_id=1, source_target_pairs={{0,8},{8,0},{1,9},{9,1},{2,10},{10,2},{3,11},{11,3},{4,12},{12,4},... | collective-permute-start | bytes 393224 | tf_op jit(solution)/shard_map/ppermute | solution.py:366
  4.9 1.5 %collective-permute-start.2 = (f32[2,16,8,128]{3,2,1,0:T(8,128)S(1)}, f32[2,16,8,128]{3,2,1,0:T(8,128)S(1)}, u32[]{:S(2)}, u32[]{:S(2)}) collective-permute-start(f32[2,16,8,128]{3,2,1,0:T(8,128)S(1)} %get-tuple-element.156), channel_id=1, source_target_pairs={{0,4},{4,0},{1,5},{5,1},{2,6},{6,2},{3,7},{7,3},{8,12},{12,8},{9,1... | collective-permute-start | bytes 393224 | tf_op jit(solution)/shard_map/ppermute | solution.py:366
  6.3 1.3 open_chunk.5
  8.4 1.4 %open_chunk.6 = (f32[32,8,8,128]{3,2,1,0:T(8,128)S(1)}, f32[8,8,128]{2,1,0:T(8,128)S(1)}, f32[8,8,128]{2,1,0:T(8,128)S(1)}, f32[2,32,8,128]{3,2,1,0:T(8,128)S(1)}, f32[2,32,8,128]{3,2,1,0:T(8,128)S(1)}) custom-call(f32[96,8,8,128]{3,2,1,0:T(8,128)} %whole.7, f32[8,8,128]{2,1,0:T(8,128)S(1)} %get-tuple-element.152.after.refs_3_), custom_call_target="tpu_custom_call" | custom-call | flops 1048576 | bytes 2097152 | tf_op jit(solution)/shard_map/open_chunk/pallas_call | solution.py:83
  9.8 1.2 open_chunk.7
  11.1 1.2 collective-permute-done.refs_2_
  12.2 1.9 %collective-permute-start.6 = (f32[2,32,8,128]{3,2,1,0:T(8,128)S(1)}, f32[2,32,8,128]{3,2,1,0:T(8,128)S(1)}, u32[]{:S(2)}, u32[]{:S(2)}) collective-permute-start(f32[2,32,8,128]{3,2,1,0:T(8,128)S(1)} %get-tuple-element.165), channel_id=1, source_target_pairs={{0,8},{8,0},{1,9},{9,1},{2,10},{10,2},{3,11},{11,3},{4,12},{12,4},... | collective-permute-start | bytes 786440 | tf_op jit(solution)/shard_map/ppermute | solution.py:366
  14.1 1.5 %collective-permute-start.7 = (f32[2,32,8,128]{3,2,1,0:T(8,128)S(1)}, f32[2,32,8,128]{3,2,1,0:T(8,128)S(1)}, u32[]{:S(2)}, u32[]{:S(2)}) collective-permute-start(f32[2,32,8,128]{3,2,1,0:T(8,128)S(1)} %get-tuple-element.166), channel_id=1, source_target_pairs={{0,4},{4,0},{1,5},{5,1},{2,6},{6,2},{3,7},{7,3},{8,12},{12,8},{9,1... | collective-permute-start | bytes 786440 | tf_op jit(solution)/shard_map/ppermute | solution.py:366
  16.1 8.4 %collective-permute-done.4.refs_4_ = f32[2,16,8,128]{3,2,1,0:T(8,128)S(1)} collective-permute-done((f32[2,16,8,128]{3,2,1,0:T(8,128)S(1)}, f32[2,16,8,128]{3,2,1,0:T(8,128)S(1)}, u32[]{:S(2)}, u32[]{:S(2)}) %collective-permute-start.4) | collective-permute-done | bytes 131104 | tf_op jit(solution)/shard_map/ppermute | solution.py:366
  25.6 1.6 %collective-permute-start.11 = (f32[2,16,8,128]{3,2,1,0:T(8,128)S(1)}, f32[2,16,8,128]{3,2,1,0:T(8,128)S(1)}, u32[]{:S(2)}, u32[]{:S(2)}) collective-permute-start(f32[2,16,8,128]{3,2,1,0:T(8,128)S(1)} %get-tuple-element.175), channel_id=1, source_target_pairs={{0,8},{8,0},{1,9},{9,1},{2,10},{10,2},{3,11},{11,3},{4,12},{12,4},... | collective-permute-start | bytes 393224 | tf_op jit(solution)/shard_map/ppermute | solution.py:366
  28.4 1.3 collective-permute-start.18
  31.9 1.6 %collective-permute-done.12.refs_5_ = f32[2,16,8,128]{3,2,1,0:T(8,128)S(1)} collective-permute-done((f32[2,16,8,128]{3,2,1,0:T(8,128)S(1)}, f32[2,16,8,128]{3,2,1,0:T(8,128)S(1)}, u32[]{:S(2)}, u32[]{:S(2)}) %collective-permute-start.12) | collective-permute-done | bytes 131104 | tf_op jit(solution)/shard_map/ppermute | solution.py:366
  34.3 1.6 %collective-permute-start.17 = (f32[2,32,8,128]{3,2,1,0:T(8,128)S(1)}, f32[2,32,8,128]{3,2,1,0:T(8,128)S(1)}, u32[]{:S(2)}, u32[]{:S(2)}) collective-permute-start(f32[2,32,8,128]{3,2,1,0:T(8,128)S(1)} %get-tuple-element.186), channel_id=1, source_target_pairs={{0,4},{4,0},{1,5},{5,1},{2,6},{6,2},{3,7},{7,3},{8,12},{12,8},{9,1... | collective-permute-start | bytes 786440 | tf_op jit(solution)/shard_map/ppermute | solution.py:366
  36.3 1.2 collective-permute-done.23.refs_3_
  37.9 1.4 %collective-permute-start.15 = (f32[2,16,8,128]{3,2,1,0:T(8,128)S(1)}, f32[2,16,8,128]{3,2,1,0:T(8,128)S(1)}, u32[]{:S(2)}, u32[]{:S(2)}) collective-permute-start(f32[2,16,8,128]{3,2,1,0:T(8,128)S(1)} %get-tuple-element.181), channel_id=1, source_target_pairs={{0,4},{4,0},{1,5},{5,1},{2,6},{6,2},{3,7},{7,3},{8,12},{12,8},{9,1... | collective-permute-start | bytes 393224 | tf_op jit(solution)/shard_map/ppermute | solution.py:366
  40.6 5.4 %collective-permute-done.14.refs_4_ = f32[2,16,8,128]{3,2,1,0:T(8,128)S(1)} collective-permute-done((f32[2,16,8,128]{3,2,1,0:T(8,128)S(1)}, f32[2,16,8,128]{3,2,1,0:T(8,128)S(1)}, u32[]{:S(2)}, u32[]{:S(2)}) %collective-permute-start.14) | collective-permute-done | bytes 131104 | tf_op jit(solution)/shard_map/ppermute | solution.py:366
  46.0 1.3 %collective-permute-start.28 = (f32[2,32,8,128]{3,2,1,0:T(8,128)S(1)}, f32[2,32,8,128]{3,2,1,0:T(8,128)S(1)}, u32[]{:S(2)}, u32[]{:S(2)}) collective-permute-start(f32[2,32,8,128]{3,2,1,0:T(8,128)S(1)} %get-tuple-element.209), channel_id=1, source_target_pairs={{0,8},{8,0},{1,9},{9,1},{2,10},{10,2},{3,11},{11,3},{4,12},{12,4},... | collective-permute-start | bytes 786440 | tf_op jit(solution)/shard_map/ppermute | solution.py:366
  48.0 1.4 %collective-permute-start.22 = (f32[2,16,8,128]{3,2,1,0:T(8,128)S(1)}, f32[2,16,8,128]{3,2,1,0:T(8,128)S(1)}, u32[]{:S(2)}, u32[]{:S(2)}) collective-permute-start(f32[2,16,8,128]{3,2,1,0:T(8,128)S(1)} %get-tuple-element.196), channel_id=1, source_target_pairs={{0,4},{4,0},{1,5},{5,1},{2,6},{6,2},{3,7},{7,3},{8,12},{12,8},{9,1... | collective-permute-start | bytes 393224 | tf_op jit(solution)/shard_map/ppermute | solution.py:366
  50.8 1.5 %collective-permute-start.27 = (f32[2,32,8,128]{3,2,1,0:T(8,128)S(1)}, f32[2,32,8,128]{3,2,1,0:T(8,128)S(1)}, u32[]{:S(2)}, u32[]{:S(2)}) collective-permute-start(f32[2,32,8,128]{3,2,1,0:T(8,128)S(1)} %get-tuple-element.206), channel_id=1, source_target_pairs={{0,4},{4,0},{1,5},{5,1},{2,6},{6,2},{3,7},{7,3},{8,12},{12,8},{9,1... | collective-permute-start | bytes 786440 | tf_op jit(solution)/shard_map/ppermute | solution.py:366
  52.6 6.1 %collective-permute-done.22.refs_5_ = f32[2,16,8,128]{3,2,1,0:T(8,128)S(1)} collective-permute-done((f32[2,16,8,128]{3,2,1,0:T(8,128)S(1)}, f32[2,16,8,128]{3,2,1,0:T(8,128)S(1)}, u32[]{:S(2)}, u32[]{:S(2)}) %collective-permute-start.22) | collective-permute-done | bytes 131104 | tf_op jit(solution)/shard_map/ppermute | solution.py:366
  58.7 1.2 collective-permute-done.20.refs_2_
  60.2 1.1 collective-permute-start.25
  61.7 1.1 collective-permute-start.31
  63.4 1.1 collective-permute-start.38
  66.3 1.5 %collective-permute-start.36 = (f32[2,32,8,128]{3,2,1,0:T(8,128)S(1)}, f32[2,32,8,128]{3,2,1,0:T(8,128)S(1)}, u32[]{:S(2)}, u32[]{:S(2)}) collective-permute-start(f32[2,32,8,128]{3,2,1,0:T(8,128)S(1)} %get-tuple-element.225), channel_id=1, source_target_pairs={{0,8},{8,0},{1,9},{9,1},{2,10},{10,2},{3,11},{11,3},{4,12},{12,4},... | collective-permute-start | bytes 786440 | tf_op jit(solution)/shard_map/ppermute | solution.py:366
  70.1 10.0 %collective-permute-done.32.refs_5_ = f32[2,16,8,128]{3,2,1,0:T(8,128)S(1)} collective-permute-done((f32[2,16,8,128]{3,2,1,0:T(8,128)S(1)}, f32[2,16,8,128]{3,2,1,0:T(8,128)S(1)}, u32[]{:S(2)}, u32[]{:S(2)}) %collective-permute-start.32) | collective-permute-done | bytes 131104 | tf_op jit(solution)/shard_map/ppermute | solution.py:366
  80.2 1.2 collective-permute-done.30.refs_2_
  81.4 1.1 collective-permute-start.34
  82.5 1.5 %collective-permute-start.35 = (f32[2,16,8,128]{3,2,1,0:T(8,128)S(1)}, f32[2,16,8,128]{3,2,1,0:T(8,128)S(1)}, u32[]{:S(2)}, u32[]{:S(2)}) collective-permute-start(f32[2,16,8,128]{3,2,1,0:T(8,128)S(1)} %get-tuple-element.221), channel_id=1, source_target_pairs={{0,4},{4,0},{1,5},{5,1},{2,6},{6,2},{3,7},{7,3},{8,12},{12,8},{9,1... | collective-permute-start | bytes 393224 | tf_op jit(solution)/shard_map/ppermute | solution.py:366
  86.0 1.7 %collective-permute-start.46 = (f32[2,32,8,128]{3,2,1,0:T(8,128)S(1)}, f32[2,32,8,128]{3,2,1,0:T(8,128)S(1)}, u32[]{:S(2)}, u32[]{:S(2)}) collective-permute-start(f32[2,32,8,128]{3,2,1,0:T(8,128)S(1)} %get-tuple-element.245), channel_id=1, source_target_pairs={{0,8},{8,0},{1,9},{9,1},{2,10},{10,2},{3,11},{11,3},{4,12},{12,4},... | collective-permute-start | bytes 786440 | tf_op jit(solution)/shard_map/ppermute | solution.py:366
  87.7 1.2 collective-permute-done.33.refs_3_
  91.3 1.1 collective-permute-start.47
  92.7 2.6 %collective-permute-done.42.refs_5_ = f32[2,16,8,128]{3,2,1,0:T(8,128)S(1)} collective-permute-done((f32[2,16,8,128]{3,2,1,0:T(8,128)S(1)}, f32[2,16,8,128]{3,2,1,0:T(8,128)S(1)}, u32[]{:S(2)}, u32[]{:S(2)}) %collective-permute-start.42) | collective-permute-done | bytes 131104 | tf_op jit(solution)/shard_map/ppermute | solution.py:366
  95.3 1.2 collective-permute-done.40.refs_2_
  97.9 4.1 %collective-permute-done.48.refs_4_ = f32[2,32,8,128]{3,2,1,0:T(8,128)S(1)} collective-permute-done((f32[2,32,8,128]{3,2,1,0:T(8,128)S(1)}, f32[2,32,8,128]{3,2,1,0:T(8,128)S(1)}, u32[]{:S(2)}, u32[]{:S(2)}) %collective-permute-start.48) | collective-permute-done | bytes 262176 | tf_op jit(solution)/shard_map/ppermute | solution.py:366
  103.9 2.6 %collective-permute-done.47.refs_5_ = f32[2,32,8,128]{3,2,1,0:T(8,128)S(1)} collective-permute-done((f32[2,32,8,128]{3,2,1,0:T(8,128)S(1)}, f32[2,32,8,128]{3,2,1,0:T(8,128)S(1)}, u32[]{:S(2)}, u32[]{:S(2)}) %collective-permute-start.47) | collective-permute-done | bytes 262176 | tf_op jit(solution)/shard_map/ppermute | solution.py:366
  109.0 1.2 collective-permute-start.64
  110.2 1.5 %collective-permute-start.63 = (f32[2,32,4,128]{3,2,1,0:T(4,128)S(1)}, f32[2,32,4,128]{3,2,1,0:T(4,128)S(1)}, u32[]{:S(2)}, u32[]{:S(2)}) collective-permute-start(f32[2,32,4,128]{3,2,1,0:T(4,128)S(1)} %get-tuple-element.286), channel_id=1, source_target_pairs={{0,4},{4,0},{1,5},{5,1},{2,6},{6,2},{3,7},{7,3},{8,12},{12,8},{9,1... | collective-permute-start | bytes 393224 | tf_op jit(solution)/shard_map/ppermute | solution.py:366
  111.8 1.8 %collective-permute-start.60 = (f32[32,8,128]{2,1,0:T(8,128)S(1)}, f32[32,8,128]{2,1,0:T(8,128)S(1)}, u32[]{:S(2)}, u32[]{:S(2)}) collective-permute-start(f32[32,8,128]{2,1,0:T(8,128)S(1)} %get-tuple-element.281), channel_id=1, source_target_pairs={{0,8},{8,0},{1,9},{9,1},{2,10},{10,2},{3,11},{11,3},{4,12},{12,4},... | collective-permute-start | bytes 393224 | tf_op jit(solution)/shard_map/ppermute | solution.py:415
  115.9 1.4 %collective-permute-start.65 = (f32[2,16,4,128]{3,2,1,0:T(4,128)S(1)}, f32[2,16,4,128]{3,2,1,0:T(4,128)S(1)}, u32[]{:S(2)}, u32[]{:S(2)}) collective-permute-start(f32[2,16,4,128]{3,2,1,0:T(4,128)S(1)} %get-tuple-element.290), channel_id=1, source_target_pairs={{0,4},{4,0},{1,5},{5,1},{2,6},{6,2},{3,7},{7,3},{8,12},{12,8},{9,1... | collective-permute-start | bytes 196616 | tf_op jit(solution)/shard_map/ppermute | solution.py:366
  118.2 1.8 %collective-permute-start.53 = (f32[32,8,128]{2,1,0:T(8,128)S(1)}, f32[32,8,128]{2,1,0:T(8,128)S(1)}, u32[]{:S(2)}, u32[]{:S(2)}) collective-permute-start(f32[32,8,128]{2,1,0:T(8,128)S(1)} %get-tuple-element.269), channel_id=1, source_target_pairs={{8,0},{0,8},{9,1},{1,9},{10,2},{2,10},{11,3},{3,11},{12,4},{4,12},... | collective-permute-start | bytes 393224 | tf_op jit(solution)/shard_map/ppermute | solution.py:415
  121.4 4.1 %collective-permute-done.65.refs_5_ = f32[2,16,4,128]{3,2,1,0:T(4,128)S(1)} collective-permute-done((f32[2,16,4,128]{3,2,1,0:T(4,128)S(1)}, f32[2,16,4,128]{3,2,1,0:T(4,128)S(1)}, u32[]{:S(2)}, u32[]{:S(2)}) %collective-permute-start.65) | collective-permute-done | bytes 65568 | tf_op jit(solution)/shard_map/ppermute | solution.py:366
  125.8 1.2 collective-permute-done.66.refs_5_
  127.3 1.1 collective-permute-start.57
  128.4 1.7 %close.2 = (f32[96,8,8,128]{3,2,1,0:T(8,128)}, f32[96,8,8,128]{3,2,1,0:T(8,128)}) custom-call(f32[16,4,8,128]{3,2,1,0:T(8,128)S(1)} %get-tuple-element.280.refs_0_, f32[32,4,8,128]{3,2,1,0:T(8,128)S(1)} %get-tuple-element.284.refs_1_, f32[32,4,8,128]{3,2,1,0:T(8,128)S(1)} %get-tuple-element.288.refs_2_, f32[16,4,8,128]{3,2,1,0:T(8,128)S(1)} %get-tuple-element.292.refs_3_, ...), custom_call_target="tpu_custom_call" | custom-call | flops 1179648 | bytes 6291456 | tf_op jit(solution)/shard_map/close/pallas_call | solution.py:344
  131.8 1.2 write_parts.1
  133.0 1.2 close.3
  (125 shorter events, 33.7 us)
Async XLA Ops:
  1.8 12.3 %collective-permute-start.1 = (f32[2,16,8,128]{3,2,1,0:T(8,128)S(1)}, f32[2,16,8,128]{3,2,1,0:T(8,128)S(1)}, u32[]{:S(2)}, u32[]{:S(2)}) collective-permute-start(f32[2,16,8,128]{3,2,1,0:T(8,128)S(1)} %get-tuple-element.155), channel_id=1, source_target_pairs={{0,8},{8,0},{1,9},{9,1},{2,10},{10,2},{3,11},{11,3},{4,12},{12,4},... | collective-permute-start | bytes 393224 | tf_op jit(solution)/shard_map/ppermute | solution.py:366
  4.9 10.8 %collective-permute-start.2 = (f32[2,16,8,128]{3,2,1,0:T(8,128)S(1)}, f32[2,16,8,128]{3,2,1,0:T(8,128)S(1)}, u32[]{:S(2)}, u32[]{:S(2)}) collective-permute-start(f32[2,16,8,128]{3,2,1,0:T(8,128)S(1)} %get-tuple-element.156), channel_id=1, source_target_pairs={{0,4},{4,0},{1,5},{5,1},{2,6},{6,2},{3,7},{7,3},{8,12},{12,8},{9,1... | collective-permute-start | bytes 393224 | tf_op jit(solution)/shard_map/ppermute | solution.py:366
  7.6 18.0 %collective-permute-start.8 = (f32[2,32,8,128]{3,2,1,0:T(8,128)S(1)}, f32[2,32,8,128]{3,2,1,0:T(8,128)S(1)}, u32[]{:S(2)}, u32[]{:S(2)}) collective-permute-start(f32[2,32,8,128]{3,2,1,0:T(8,128)S(1)} %get-tuple-element.169), channel_id=1, source_target_pairs={{0,8},{8,0},{1,9},{9,1},{2,10},{10,2},{3,11},{11,3},{4,12},{12,4},... | collective-permute-start | bytes 786440 | tf_op jit(solution)/shard_map/ppermute | solution.py:366
  8.2 19.0 %collective-permute-start.9 = (f32[2,32,8,128]{3,2,1,0:T(8,128)S(1)}, f32[2,32,8,128]{3,2,1,0:T(8,128)S(1)}, u32[]{:S(2)}, u32[]{:S(2)}) collective-permute-start(f32[2,32,8,128]{3,2,1,0:T(8,128)S(1)} %get-tuple-element.170), channel_id=1, source_target_pairs={{0,4},{4,0},{1,5},{5,1},{2,6},{6,2},{3,7},{7,3},{8,12},{12,8},{9,1... | collective-permute-start | bytes 786440 | tf_op jit(solution)/shard_map/ppermute | solution.py:366
  12.2 16.1 %collective-permute-start.6 = (f32[2,32,8,128]{3,2,1,0:T(8,128)S(1)}, f32[2,32,8,128]{3,2,1,0:T(8,128)S(1)}, u32[]{:S(2)}, u32[]{:S(2)}) collective-permute-start(f32[2,32,8,128]{3,2,1,0:T(8,128)S(1)} %get-tuple-element.165), channel_id=1, source_target_pairs={{0,8},{8,0},{1,9},{9,1},{2,10},{10,2},{3,11},{11,3},{4,12},{12,4},... | collective-permute-start | bytes 786440 | tf_op jit(solution)/shard_map/ppermute | solution.py:366
  14.1 15.6 %collective-permute-start.7 = (f32[2,32,8,128]{3,2,1,0:T(8,128)S(1)}, f32[2,32,8,128]{3,2,1,0:T(8,128)S(1)}, u32[]{:S(2)}, u32[]{:S(2)}) collective-permute-start(f32[2,32,8,128]{3,2,1,0:T(8,128)S(1)} %get-tuple-element.166), channel_id=1, source_target_pairs={{0,4},{4,0},{1,5},{5,1},{2,6},{6,2},{3,7},{7,3},{8,12},{12,8},{9,1... | collective-permute-start | bytes 786440 | tf_op jit(solution)/shard_map/ppermute | solution.py:366
  15.6 8.9 %collective-permute-start.4 = (f32[2,16,8,128]{3,2,1,0:T(8,128)S(1)}, f32[2,16,8,128]{3,2,1,0:T(8,128)S(1)}, u32[]{:S(2)}, u32[]{:S(2)}) collective-permute-start(f32[2,16,8,128]{3,2,1,0:T(8,128)S(1)} %get-tuple-element.160), channel_id=1, source_target_pairs={{0,8},{8,0},{1,9},{9,1},{2,10},{10,2},{3,11},{11,3},{4,12},{12,4},... | collective-permute-start | bytes 393224 | tf_op jit(solution)/shard_map/ppermute | solution.py:366
  24.6 6.5 %collective-permute-start.5 = (f32[2,16,8,128]{3,2,1,0:T(8,128)S(1)}, f32[2,16,8,128]{3,2,1,0:T(8,128)S(1)}, u32[]{:S(2)}, u32[]{:S(2)}) collective-permute-start(f32[2,16,8,128]{3,2,1,0:T(8,128)S(1)} %get-tuple-element.161), channel_id=1, source_target_pairs={{0,4},{4,0},{1,5},{5,1},{2,6},{6,2},{3,7},{7,3},{8,12},{12,8},{9,1... | collective-permute-start | bytes 393224 | tf_op jit(solution)/shard_map/ppermute | solution.py:366
  27.2 6.4 %collective-permute-start.12 = (f32[2,16,8,128]{3,2,1,0:T(8,128)S(1)}, f32[2,16,8,128]{3,2,1,0:T(8,128)S(1)}, u32[]{:S(2)}, u32[]{:S(2)}) collective-permute-start(f32[2,16,8,128]{3,2,1,0:T(8,128)S(1)} %get-tuple-element.176), channel_id=1, source_target_pairs={{0,4},{4,0},{1,5},{5,1},{2,6},{6,2},{3,7},{7,3},{8,12},{12,8},{9,1... | collective-permute-start | bytes 393224 | tf_op jit(solution)/shard_map/ppermute | solution.py:366
  28.4 9.5 %collective-permute-start.18 = (f32[2,32,8,128]{3,2,1,0:T(8,128)S(1)}, f32[2,32,8,128]{3,2,1,0:T(8,128)S(1)}, u32[]{:S(2)}, u32[]{:S(2)}) collective-permute-start(f32[2,32,8,128]{3,2,1,0:T(8,128)S(1)} %get-tuple-element.189), channel_id=1, source_target_pairs={{0,8},{8,0},{1,9},{9,1},{2,10},{10,2},{3,11},{11,3},{4,12},{12,4},... | collective-permute-start | bytes 786440 | tf_op jit(solution)/shard_map/ppermute | solution.py:366
  29.7 9.5 %collective-permute-start.19 = (f32[2,32,8,128]{3,2,1,0:T(8,128)S(1)}, f32[2,32,8,128]{3,2,1,0:T(8,128)S(1)}, u32[]{:S(2)}, u32[]{:S(2)}) collective-permute-start(f32[2,32,8,128]{3,2,1,0:T(8,128)S(1)} %get-tuple-element.190), channel_id=1, source_target_pairs={{0,4},{4,0},{1,5},{5,1},{2,6},{6,2},{3,7},{7,3},{8,12},{12,8},{9,1... | collective-permute-start | bytes 786440 | tf_op jit(solution)/shard_map/ppermute | solution.py:366
  33.6 13.8 %collective-permute-start.16 = (f32[2,32,8,128]{3,2,1,0:T(8,128)S(1)}, f32[2,32,8,128]{3,2,1,0:T(8,128)S(1)}, u32[]{:S(2)}, u32[]{:S(2)}) collective-permute-start(f32[2,32,8,128]{3,2,1,0:T(8,128)S(1)} %get-tuple-element.185), channel_id=1, source_target_pairs={{0,8},{8,0},{1,9},{9,1},{2,10},{10,2},{3,11},{11,3},{4,12},{12,4},... | collective-permute-start | bytes 786440 | tf_op jit(solution)/shard_map/ppermute | solution.py:366
  34.3 13.7 %collective-permute-start.17 = (f32[2,32,8,128]{3,2,1,0:T(8,128)S(1)}, f32[2,32,8,128]{3,2,1,0:T(8,128)S(1)}, u32[]{:S(2)}, u32[]{:S(2)}) collective-permute-start(f32[2,32,8,128]{3,2,1,0:T(8,128)S(1)} %get-tuple-element.186), channel_id=1, source_target_pairs={{0,4},{4,0},{1,5},{5,1},{2,6},{6,2},{3,7},{7,3},{8,12},{12,8},{9,1... | collective-permute-start | bytes 786440 | tf_op jit(solution)/shard_map/ppermute | solution.py:366
  37.5 8.5 %collective-permute-start.14 = (f32[2,16,8,128]{3,2,1,0:T(8,128)S(1)}, f32[2,16,8,128]{3,2,1,0:T(8,128)S(1)}, u32[]{:S(2)}, u32[]{:S(2)}) collective-permute-start(f32[2,16,8,128]{3,2,1,0:T(8,128)S(1)} %get-tuple-element.180), channel_id=1, source_target_pairs={{0,8},{8,0},{1,9},{9,1},{2,10},{10,2},{3,11},{11,3},{4,12},{12,4},... | collective-permute-start | bytes 393224 | tf_op jit(solution)/shard_map/ppermute | solution.py:366
  37.9 12.2 %collective-permute-start.15 = (f32[2,16,8,128]{3,2,1,0:T(8,128)S(1)}, f32[2,16,8,128]{3,2,1,0:T(8,128)S(1)}, u32[]{:S(2)}, u32[]{:S(2)}) collective-permute-start(f32[2,16,8,128]{3,2,1,0:T(8,128)S(1)} %get-tuple-element.181), channel_id=1, source_target_pairs={{0,4},{4,0},{1,5},{5,1},{2,6},{6,2},{3,7},{7,3},{8,12},{12,8},{9,1... | collective-permute-start | bytes 393224 | tf_op jit(solution)/shard_map/ppermute | solution.py:366
  39.2 11.5 %collective-permute-start.21 = (f32[2,16,8,128]{3,2,1,0:T(8,128)S(1)}, f32[2,16,8,128]{3,2,1,0:T(8,128)S(1)}, u32[]{:S(2)}, u32[]{:S(2)}) collective-permute-start(f32[2,16,8,128]{3,2,1,0:T(8,128)S(1)} %get-tuple-element.195), channel_id=1, source_target_pairs={{0,8},{8,0},{1,9},{9,1},{2,10},{10,2},{3,11},{11,3},{4,12},{12,4},... | collective-permute-start | bytes 393224 | tf_op jit(solution)/shard_map/ppermute | solution.py:366
  46.0 14.2 %collective-permute-start.28 = (f32[2,32,8,128]{3,2,1,0:T(8,128)S(1)}, f32[2,32,8,128]{3,2,1,0:T(8,128)S(1)}, u32[]{:S(2)}, u32[]{:S(2)}) collective-permute-start(f32[2,32,8,128]{3,2,1,0:T(8,128)S(1)} %get-tuple-element.209), channel_id=1, source_target_pairs={{0,8},{8,0},{1,9},{9,1},{2,10},{10,2},{3,11},{11,3},{4,12},{12,4},... | collective-permute-start | bytes 786440 | tf_op jit(solution)/shard_map/ppermute | solution.py:366
  47.4 14.3 %collective-permute-start.29 = (f32[2,32,8,128]{3,2,1,0:T(8,128)S(1)}, f32[2,32,8,128]{3,2,1,0:T(8,128)S(1)}, u32[]{:S(2)}, u32[]{:S(2)}) collective-permute-start(f32[2,32,8,128]{3,2,1,0:T(8,128)S(1)} %get-tuple-element.210), channel_id=1, source_target_pairs={{0,4},{4,0},{1,5},{5,1},{2,6},{6,2},{3,7},{7,3},{8,12},{12,8},{9,1... | collective-permute-start | bytes 786440 | tf_op jit(solution)/shard_map/ppermute | solution.py:366
  48.0 10.7 %collective-permute-start.22 = (f32[2,16,8,128]{3,2,1,0:T(8,128)S(1)}, f32[2,16,8,128]{3,2,1,0:T(8,128)S(1)}, u32[]{:S(2)}, u32[]{:S(2)}) collective-permute-start(f32[2,16,8,128]{3,2,1,0:T(8,128)S(1)} %get-tuple-element.196), channel_id=1, source_target_pairs={{0,4},{4,0},{1,5},{5,1},{2,6},{6,2},{3,7},{7,3},{8,12},{12,8},{9,1... | collective-permute-start | bytes 393224 | tf_op jit(solution)/shard_map/ppermute | solution.py:366
  50.0 13.3 %collective-permute-start.26 = (f32[2,32,8,128]{3,2,1,0:T(8,128)S(1)}, f32[2,32,8,128]{3,2,1,0:T(8,128)S(1)}, u32[]{:S(2)}, u32[]{:S(2)}) collective-permute-start(f32[2,32,8,128]{3,2,1,0:T(8,128)S(1)} %get-tuple-element.205), channel_id=1, source_target_pairs={{0,8},{8,0},{1,9},{9,1},{2,10},{10,2},{3,11},{11,3},{4,12},{12,4},... | collective-permute-start | bytes 786440 | tf_op jit(solution)/shard_map/ppermute | solution.py:366
  50.8 13.7 %collective-permute-start.27 = (f32[2,32,8,128]{3,2,1,0:T(8,128)S(1)}, f32[2,32,8,128]{3,2,1,0:T(8,128)S(1)}, u32[]{:S(2)}, u32[]{:S(2)}) collective-permute-start(f32[2,32,8,128]{3,2,1,0:T(8,128)S(1)} %get-tuple-element.206), channel_id=1, source_target_pairs={{0,4},{4,0},{1,5},{5,1},{2,6},{6,2},{3,7},{7,3},{8,12},{12,8},{9,1... | collective-permute-start | bytes 786440 | tf_op jit(solution)/shard_map/ppermute | solution.py:366
  59.9 6.4 %collective-permute-start.24 = (f32[2,16,8,128]{3,2,1,0:T(8,128)S(1)}, f32[2,16,8,128]{3,2,1,0:T(8,128)S(1)}, u32[]{:S(2)}, u32[]{:S(2)}) collective-permute-start(f32[2,16,8,128]{3,2,1,0:T(8,128)S(1)} %get-tuple-element.200), channel_id=1, source_target_pairs={{0,8},{8,0},{1,9},{9,1},{2,10},{10,2},{3,11},{11,3},{4,12},{12,4},... | collective-permute-start | bytes 393224 | tf_op jit(solution)/shard_map/ppermute | solution.py:366
  60.2 7.5 %collective-permute-start.25 = (f32[2,16,8,128]{3,2,1,0:T(8,128)S(1)}, f32[2,16,8,128]{3,2,1,0:T(8,128)S(1)}, u32[]{:S(2)}, u32[]{:S(2)}) collective-permute-start(f32[2,16,8,128]{3,2,1,0:T(8,128)S(1)} %get-tuple-element.201), channel_id=1, source_target_pairs={{0,4},{4,0},{1,5},{5,1},{2,6},{6,2},{3,7},{7,3},{8,12},{12,8},{9,1... | collective-permute-start | bytes 393224 | tf_op jit(solution)/shard_map/ppermute | solution.py:366
  61.7 7.4 %collective-permute-start.31 = (f32[2,16,8,128]{3,2,1,0:T(8,128)S(1)}, f32[2,16,8,128]{3,2,1,0:T(8,128)S(1)}, u32[]{:S(2)}, u32[]{:S(2)}) collective-permute-start(f32[2,16,8,128]{3,2,1,0:T(8,128)S(1)} %get-tuple-element.215), channel_id=1, source_target_pairs={{0,8},{8,0},{1,9},{9,1},{2,10},{10,2},{3,11},{11,3},{4,12},{12,4},... | collective-permute-start | bytes 393224 | tf_op jit(solution)/shard_map/ppermute | solution.py:366
  63.4 19.1 %collective-permute-start.38 = (f32[2,32,8,128]{3,2,1,0:T(8,128)S(1)}, f32[2,32,8,128]{3,2,1,0:T(8,128)S(1)}, u32[]{:S(2)}, u32[]{:S(2)}) collective-permute-start(f32[2,32,8,128]{3,2,1,0:T(8,128)S(1)} %get-tuple-element.229), channel_id=1, source_target_pairs={{0,8},{8,0},{1,9},{9,1},{2,10},{10,2},{3,11},{11,3},{4,12},{12,4},... | collective-permute-start | bytes 786440 | tf_op jit(solution)/shard_map/ppermute | solution.py:366
  64.5 19.8 %collective-permute-start.39 = (f32[2,32,8,128]{3,2,1,0:T(8,128)S(1)}, f32[2,32,8,128]{3,2,1,0:T(8,128)S(1)}, u32[]{:S(2)}, u32[]{:S(2)}) collective-permute-start(f32[2,32,8,128]{3,2,1,0:T(8,128)S(1)} %get-tuple-element.230), channel_id=1, source_target_pairs={{0,4},{4,0},{1,5},{5,1},{2,6},{6,2},{3,7},{7,3},{8,12},{12,8},{9,1... | collective-permute-start | bytes 786440 | tf_op jit(solution)/shard_map/ppermute | solution.py:366
  66.3 19.1 %collective-permute-start.36 = (f32[2,32,8,128]{3,2,1,0:T(8,128)S(1)}, f32[2,32,8,128]{3,2,1,0:T(8,128)S(1)}, u32[]{:S(2)}, u32[]{:S(2)}) collective-permute-start(f32[2,32,8,128]{3,2,1,0:T(8,128)S(1)} %get-tuple-element.225), channel_id=1, source_target_pairs={{0,8},{8,0},{1,9},{9,1},{2,10},{10,2},{3,11},{11,3},{4,12},{12,4},... | collective-permute-start | bytes 786440 | tf_op jit(solution)/shard_map/ppermute | solution.py:366
  67.8 17.6 %collective-permute-start.37 = (f32[2,32,8,128]{3,2,1,0:T(8,128)S(1)}, f32[2,32,8,128]{3,2,1,0:T(8,128)S(1)}, u32[]{:S(2)}, u32[]{:S(2)}) collective-permute-start(f32[2,32,8,128]{3,2,1,0:T(8,128)S(1)} %get-tuple-element.226), channel_id=1, source_target_pairs={{0,4},{4,0},{1,5},{5,1},{2,6},{6,2},{3,7},{7,3},{8,12},{12,8},{9,1... | collective-permute-start | bytes 786440 | tf_op jit(solution)/shard_map/ppermute | solution.py:366
  69.1 11.1 %collective-permute-start.32 = (f32[2,16,8,128]{3,2,1,0:T(8,128)S(1)}, f32[2,16,8,128]{3,2,1,0:T(8,128)S(1)}, u32[]{:S(2)}, u32[]{:S(2)}) collective-permute-start(f32[2,16,8,128]{3,2,1,0:T(8,128)S(1)} %get-tuple-element.216), channel_id=1, source_target_pairs={{0,4},{4,0},{1,5},{5,1},{2,6},{6,2},{3,7},{7,3},{8,12},{12,8},{9,1... | collective-permute-start | bytes 393224 | tf_op jit(solution)/shard_map/ppermute | solution.py:366
  81.4 8.1 %collective-permute-start.34 = (f32[2,16,8,128]{3,2,1,0:T(8,128)S(1)}, f32[2,16,8,128]{3,2,1,0:T(8,128)S(1)}, u32[]{:S(2)}, u32[]{:S(2)}) collective-permute-start(f32[2,16,8,128]{3,2,1,0:T(8,128)S(1)} %get-tuple-element.220), channel_id=1, source_target_pairs={{0,8},{8,0},{1,9},{9,1},{2,10},{10,2},{3,11},{11,3},{4,12},{12,4},... | collective-permute-start | bytes 393224 | tf_op jit(solution)/shard_map/ppermute | solution.py:366
  82.5 7.9 %collective-permute-start.35 = (f32[2,16,8,128]{3,2,1,0:T(8,128)S(1)}, f32[2,16,8,128]{3,2,1,0:T(8,128)S(1)}, u32[]{:S(2)}, u32[]{:S(2)}) collective-permute-start(f32[2,16,8,128]{3,2,1,0:T(8,128)S(1)} %get-tuple-element.221), channel_id=1, source_target_pairs={{0,4},{4,0},{1,5},{5,1},{2,6},{6,2},{3,7},{7,3},{8,12},{12,8},{9,1... | collective-permute-start | bytes 393224 | tf_op jit(solution)/shard_map/ppermute | solution.py:366
  84.3 7.0 %collective-permute-start.41 = (f32[2,16,8,128]{3,2,1,0:T(8,128)S(1)}, f32[2,16,8,128]{3,2,1,0:T(8,128)S(1)}, u32[]{:S(2)}, u32[]{:S(2)}) collective-permute-start(f32[2,16,8,128]{3,2,1,0:T(8,128)S(1)} %get-tuple-element.235), channel_id=1, source_target_pairs={{0,8},{8,0},{1,9},{9,1},{2,10},{10,2},{3,11},{11,3},{4,12},{12,4},... | collective-permute-start | bytes 393224 | tf_op jit(solution)/shard_map/ppermute | solution.py:366
  86.0 10.9 %collective-permute-start.46 = (f32[2,32,8,128]{3,2,1,0:T(8,128)S(1)}, f32[2,32,8,128]{3,2,1,0:T(8,128)S(1)}, u32[]{:S(2)}, u32[]{:S(2)}) collective-permute-start(f32[2,32,8,128]{3,2,1,0:T(8,128)S(1)} %get-tuple-element.245), channel_id=1, source_target_pairs={{0,8},{8,0},{1,9},{9,1},{2,10},{10,2},{3,11},{11,3},{4,12},{12,4},... | collective-permute-start | bytes 786440 | tf_op jit(solution)/shard_map/ppermute | solution.py:366
  88.9 6.4 %collective-permute-start.42 = (f32[2,16,8,128]{3,2,1,0:T(8,128)S(1)}, f32[2,16,8,128]{3,2,1,0:T(8,128)S(1)}, u32[]{:S(2)}, u32[]{:S(2)}) collective-permute-start(f32[2,16,8,128]{3,2,1,0:T(8,128)S(1)} %get-tuple-element.236), channel_id=1, source_target_pairs={{0,4},{4,0},{1,5},{5,1},{2,6},{6,2},{3,7},{7,3},{8,12},{12,8},{9,1... | collective-permute-start | bytes 393224 | tf_op jit(solution)/shard_map/ppermute | solution.py:366
  89.4 12.5 %collective-permute-start.48 = (f32[2,32,8,128]{3,2,1,0:T(8,128)S(1)}, f32[2,32,8,128]{3,2,1,0:T(8,128)S(1)}, u32[]{:S(2)}, u32[]{:S(2)}) collective-permute-start(f32[2,32,8,128]{3,2,1,0:T(8,128)S(1)} %get-tuple-element.249), channel_id=1, source_target_pairs={{0,8},{8,0},{1,9},{9,1},{2,10},{10,2},{3,11},{11,3},{4,12},{12,4},... | collective-permute-start | bytes 786440 | tf_op jit(solution)/shard_map/ppermute | solution.py:366
  90.4 11.9 %collective-permute-start.49 = (f32[2,32,8,128]{3,2,1,0:T(8,128)S(1)}, f32[2,32,8,128]{3,2,1,0:T(8,128)S(1)}, u32[]{:S(2)}, u32[]{:S(2)}) collective-permute-start(f32[2,32,8,128]{3,2,1,0:T(8,128)S(1)} %get-tuple-element.250), channel_id=1, source_target_pairs={{0,4},{4,0},{1,5},{5,1},{2,6},{6,2},{3,7},{7,3},{8,12},{12,8},{9,1... | collective-permute-start | bytes 786440 | tf_op jit(solution)/shard_map/ppermute | solution.py:366
  91.3 15.2 %collective-permute-start.47 = (f32[2,32,8,128]{3,2,1,0:T(8,128)S(1)}, f32[2,32,8,128]{3,2,1,0:T(8,128)S(1)}, u32[]{:S(2)}, u32[]{:S(2)}) collective-permute-start(f32[2,32,8,128]{3,2,1,0:T(8,128)S(1)} %get-tuple-element.246), channel_id=1, source_target_pairs={{0,4},{4,0},{1,5},{5,1},{2,6},{6,2},{3,7},{7,3},{8,12},{12,8},{9,1... | collective-permute-start | bytes 786440 | tf_op jit(solution)/shard_map/ppermute | solution.py:366
  96.5 11.1 %collective-permute-start.44 = (f32[2,16,8,128]{3,2,1,0:T(8,128)S(1)}, f32[2,16,8,128]{3,2,1,0:T(8,128)S(1)}, u32[]{:S(2)}, u32[]{:S(2)}) collective-permute-start(f32[2,16,8,128]{3,2,1,0:T(8,128)S(1)} %get-tuple-element.240), channel_id=1, source_target_pairs={{0,8},{8,0},{1,9},{9,1},{2,10},{10,2},{3,11},{11,3},{4,12},{12,4},... | collective-permute-start | bytes 393224 | tf_op jit(solution)/shard_map/ppermute | solution.py:366
  96.9 11.8 %collective-permute-start.45 = (f32[2,16,8,128]{3,2,1,0:T(8,128)S(1)}, f32[2,16,8,128]{3,2,1,0:T(8,128)S(1)}, u32[]{:S(2)}, u32[]{:S(2)}) collective-permute-start(f32[2,16,8,128]{3,2,1,0:T(8,128)S(1)} %get-tuple-element.241), channel_id=1, source_target_pairs={{0,4},{4,0},{1,5},{5,1},{2,6},{6,2},{3,7},{7,3},{8,12},{12,8},{9,1... | collective-permute-start | bytes 393224 | tf_op jit(solution)/shard_map/ppermute | solution.py:366
  102.3 9.4 %collective-permute-start.58 = (f32[16,8,128]{2,1,0:T(8,128)S(1)}, f32[16,8,128]{2,1,0:T(8,128)S(1)}, u32[]{:S(2)}, u32[]{:S(2)}) collective-permute-start(f32[16,8,128]{2,1,0:T(8,128)S(1)} %get-tuple-element.278), channel_id=1, source_target_pairs={{0,8},{8,0},{1,9},{9,1},{2,10},{10,2},{3,11},{11,3},{4,12},{12,4},... | collective-permute-start | bytes 196616 | tf_op jit(solution)/shard_map/ppermute | solution.py:415
  107.1 7.8 %collective-permute-start.62 = (f32[32,8,128]{2,1,0:T(8,128)S(1)}, f32[32,8,128]{2,1,0:T(8,128)S(1)}, u32[]{:S(2)}, u32[]{:S(2)}) collective-permute-start(f32[32,8,128]{2,1,0:T(8,128)S(1)} %get-tuple-element.285), channel_id=1, source_target_pairs={{0,8},{8,0},{1,9},{9,1},{2,10},{10,2},{3,11},{11,3},{4,12},{12,4},... | collective-permute-start | bytes 393224 | tf_op jit(solution)/shard_map/ppermute | solution.py:415
  111.8 6.4 %collective-permute-start.60 = (f32[32,8,128]{2,1,0:T(8,128)S(1)}, f32[32,8,128]{2,1,0:T(8,128)S(1)}, u32[]{:S(2)}, u32[]{:S(2)}) collective-permute-start(f32[32,8,128]{2,1,0:T(8,128)S(1)} %get-tuple-element.281), channel_id=1, source_target_pairs={{0,8},{8,0},{1,9},{9,1},{2,10},{10,2},{3,11},{11,3},{4,12},{12,4},... | collective-permute-start | bytes 393224 | tf_op jit(solution)/shard_map/ppermute | solution.py:415
  113.7 6.4 %collective-permute-start.61 = (f32[2,32,4,128]{3,2,1,0:T(4,128)S(1)}, f32[2,32,4,128]{3,2,1,0:T(4,128)S(1)}, u32[]{:S(2)}, u32[]{:S(2)}) collective-permute-start(f32[2,32,4,128]{3,2,1,0:T(4,128)S(1)} %get-tuple-element.282), channel_id=1, source_target_pairs={{0,4},{4,0},{1,5},{5,1},{2,6},{6,2},{3,7},{7,3},{8,12},{12,8},{9,1... | collective-permute-start | bytes 393224 | tf_op jit(solution)/shard_map/ppermute | solution.py:366
  114.5 12.8 %collective-permute-start.51 = (f32[48,8,128]{2,1,0:T(8,128)S(1)}, f32[48,8,128]{2,1,0:T(8,128)S(1)}, u32[]{:S(2)}, u32[]{:S(2)}) collective-permute-start(f32[48,8,128]{2,1,0:T(8,128)S(1)} %get-tuple-element.259), channel_id=1, source_target_pairs={{8,0},{0,8},{9,1},{1,9},{10,2},{2,10},{11,3},{3,11},{12,4},{4,12},... | collective-permute-start | bytes 589832 | tf_op jit(solution)/shard_map/ppermute | solution.py:415
  114.9 15.3 %collective-permute-start.52 = (f32[2,48,4,128]{3,2,1,0:T(4,128)S(1)}, f32[2,48,4,128]{3,2,1,0:T(4,128)S(1)}, u32[]{:S(2)}, u32[]{:S(2)}) collective-permute-start(f32[2,48,4,128]{3,2,1,0:T(4,128)S(1)} %get-tuple-element.260), channel_id=1, source_target_pairs={{0,4},{4,0},{1,5},{5,1},{2,6},{6,2},{3,7},{7,3},{8,12},{12,8},{9,1... | collective-permute-start | bytes 589832 | tf_op jit(solution)/shard_map/ppermute | solution.py:366
  115.9 9.5 %collective-permute-start.65 = (f32[2,16,4,128]{3,2,1,0:T(4,128)S(1)}, f32[2,16,4,128]{3,2,1,0:T(4,128)S(1)}, u32[]{:S(2)}, u32[]{:S(2)}) collective-permute-start(f32[2,16,4,128]{3,2,1,0:T(4,128)S(1)} %get-tuple-element.290), channel_id=1, source_target_pairs={{0,4},{4,0},{1,5},{5,1},{2,6},{6,2},{3,7},{7,3},{8,12},{12,8},{9,1... | collective-permute-start | bytes 196616 | tf_op jit(solution)/shard_map/ppermute | solution.py:366
  118.2 12.6 %collective-permute-start.53 = (f32[32,8,128]{2,1,0:T(8,128)S(1)}, f32[32,8,128]{2,1,0:T(8,128)S(1)}, u32[]{:S(2)}, u32[]{:S(2)}) collective-permute-start(f32[32,8,128]{2,1,0:T(8,128)S(1)} %get-tuple-element.269), channel_id=1, source_target_pairs={{8,0},{0,8},{9,1},{1,9},{10,2},{2,10},{11,3},{3,11},{12,4},{4,12},... | collective-permute-start | bytes 393224 | tf_op jit(solution)/shard_map/ppermute | solution.py:415
  120.1 10.7 %collective-permute-start.54 = (f32[2,32,4,128]{3,2,1,0:T(4,128)S(1)}, f32[2,32,4,128]{3,2,1,0:T(4,128)S(1)}, u32[]{:S(2)}, u32[]{:S(2)}) collective-permute-start(f32[2,32,4,128]{3,2,1,0:T(4,128)S(1)} %get-tuple-element.270), channel_id=1, source_target_pairs={{0,4},{4,0},{1,5},{5,1},{2,6},{6,2},{3,7},{7,3},{8,12},{12,8},{9,1... | collective-permute-start | bytes 393224 | tf_op jit(solution)/shard_map/ppermute | solution.py:366
  (21 other events, 81.5 us)
